TPU v7x, 256 devices: a whole 4x4x8 slice. The times are simulated.
256 devices in a mesh: mem: 16 (over y, x), gx: 4 (over z_hi, core), gy: 4 (over z_lo).
Axes of the slice: x: 4, y: 4, z: 8 (z_hi: 2, z_lo: 4; z = z_hi * 4 + z_lo), core: 2. Of those that a mesh axis runs over, the one named last changes fastest.
Arguments:
- field: bfloat16 [16, 512, 512, 128], P('mem', 'gx', 'gy'), may hold values from -6 to 6
- spectral: bfloat16 [3, 32, 2, 32, 128, 128], P(None, ('gx', 'gy'), None, None, 'mem'), may hold values from -0.0546875 to 0.0546875
- pointwise: bfloat16 [3, 128, 128], replicated, may hold values from -0.5 to 0.5
- bias: float32 [3, 128], replicated, may hold values from -3 to 3
Outputs:
- field_out: bfloat16 [16, 512, 512, 128], P('mem', 'gx', 'gy')
All inputs are finite; a program needn't handle non-finite values.
Results may differ from a plain program's by a relative error of at most 0.02.
Values may be sent and summed in bfloat16 or wider, within the bound.
No kernel may reach another device: no remote copies, remote signals or barrier semaphores. Data moves between devices by JAX's collectives and lax.ppermute only.
A program may use at most 128 MiB of HBM per device.

v0:
```python
import math

import jax
import jax.numpy as jnp
from jax import lax
from jax.sharding import PartitionSpec as P

KX = 32
KY = 32
NX = 512
NY = 512
LAYERS = 3


def split_up(x, dim, devices):
    lengths = x.shape
    blocks = x.reshape(*lengths[:dim], devices, lengths[dim] // devices, *lengths[dim + 1 :])
    return jnp.moveaxis(blocks, dim, 0)


def sent_and_summed(x, axis, dim):
    blocks = split_up(x, dim, lax.axis_size(axis))
    arrived = lax.all_to_all(blocks, axis, split_axis=0, concat_axis=0, tiled=True)
    return arrived.astype(jnp.float32).sum(axis=0)


def from_everyone(x, axis):
    copies = jnp.broadcast_to(x, (lax.axis_size(axis), *x.shape))
    return lax.all_to_all(copies, axis, split_axis=0, concat_axis=0, tiled=True)


def joined_along(blocks, dim):
    lengths = list(blocks.shape[1:])
    lengths[dim] *= blocks.shape[0]
    return jnp.moveaxis(blocks, 0, dim).reshape(lengths)


def collect(x, axis, dim):
    blocks = from_everyone(x, axis)
    return joined_along(blocks, dim)


def phase_angles(frequency, position, period):
    product = frequency[:, None] * position[None, :] % period
    return 2.0 * math.pi / period * product.astype(jnp.float32)


def mode_product(coeffs, weights):
    real_part = jnp.einsum(
        "...kqi,kqio->...kqo",
        coeffs[..., 0, :, :],
        weights[:, 0],
        preferred_element_type=jnp.float32,
    ) - jnp.einsum(
        "...kqi,kqio->...kqo",
        coeffs[..., 1, :, :],
        weights[:, 1],
        preferred_element_type=jnp.float32,
    )
    imag_part = jnp.einsum(
        "...kqi,kqio->...kqo",
        coeffs[..., 0, :, :],
        weights[:, 1],
        preferred_element_type=jnp.float32,
    ) + jnp.einsum(
        "...kqi,kqio->...kqo",
        coeffs[..., 1, :, :],
        weights[:, 0],
        preferred_element_type=jnp.float32,
    )
    return jnp.stack([real_part, imag_part], axis=-3)


def local(field, spectral, pointwise, bias):
    state = field[0]
    rows_here = state.shape[0]
    cols_here = state.shape[1]
    channels = state.shape[2]
    row_anchor = lax.axis_index("gx") * rows_here
    col_anchor = lax.axis_index("gy") * cols_here
    positions_x = row_anchor + jnp.arange(rows_here, dtype=jnp.int32)
    positions_y = col_anchor + jnp.arange(cols_here, dtype=jnp.int32)
    index_x = jnp.arange(KX, dtype=jnp.int32)
    freq_x = jnp.where(index_x < KX // 2, index_x, NX - KX + index_x)
    angles_y = phase_angles(jnp.arange(KY, dtype=jnp.int32), positions_y, NY)
    cosine_y = jnp.cos(angles_y).T.astype(jnp.bfloat16)
    sine_y = jnp.sin(angles_y).T.astype(jnp.bfloat16)
    forward_y = jnp.concatenate(
        [jnp.concatenate([cosine_y, -sine_y], axis=1), jnp.concatenate([sine_y, cosine_y], axis=1)],
        axis=0,
    )
    doubling = jnp.where(jnp.arange(KY) == 0, 1.0, 2.0).astype(jnp.float32)[:, None]
    wcos = doubling * jnp.cos(angles_y)
    wsin = doubling * jnp.sin(angles_y)
    inverse_y = jnp.concatenate(
        [jnp.concatenate([wcos, wsin], axis=1), jnp.concatenate([-wsin, wcos], axis=1)], axis=0
    ).astype(jnp.bfloat16)
    scale_fwd = 1.0 / math.sqrt(NX * NY)
    scale_inv = 1.0 / math.sqrt(2 * KX * KY)
    own_rows = KX // lax.axis_size(("gx", "gy"))

    def x_table():
        angles = phase_angles(freq_x, positions_x, NX)
        return (jnp.cos(angles).astype(jnp.bfloat16), jnp.sin(angles).astype(jnp.bfloat16))

    for level in range(LAYERS):
        current = state
        cosine_x, sine_x = x_table()
        table_x = jnp.concatenate([cosine_x, -sine_x], axis=0)
        partial_x = jnp.einsum(
            "kx,xyc->kyc", table_x, current, preferred_element_type=jnp.float32
        ).astype(jnp.bfloat16)
        joined = jnp.concatenate(
            [
                partial_x[: own_rows * lax.axis_size(("gx", "gy"))],
                partial_x[own_rows * lax.axis_size(("gx", "gy")) :],
            ],
            axis=1,
        )
        modes = jnp.einsum("kyc,yq->kqc", joined, forward_y, preferred_element_type=jnp.float32)
        summed = sent_and_summed(
            (modes * scale_fwd)
            .reshape(own_rows * lax.axis_size(("gx", "gy")), 2, KY, channels)
            .astype(jnp.bfloat16),
            ("gx", "gy"),
            0,
        )
        coeffs = summed.astype(jnp.bfloat16)
        weights_here = spectral[level]
        product = mode_product(coeffs, lax.all_gather(weights_here, "mem", axis=3, tiled=True))
        mixed_modes = product.astype(jnp.bfloat16)
        portion = collect(mixed_modes, ("gx", "gy"), 0)
        row_count = portion.shape[0]
        flattened = portion.reshape(row_count, 2 * KY, channels)
        qmix = jnp.einsum(
            "kqc,qy->kyc", flattened, inverse_y, preferred_element_type=jnp.float32
        ).astype(jnp.bfloat16)
        stacked = jnp.concatenate([qmix[:, :cols_here], qmix[:, cols_here:]], axis=0)
        add_cosine_x, add_sine_x = x_table()
        add_table_x = jnp.concatenate([add_cosine_x, -add_sine_x], axis=0).T
        spatial = jnp.einsum(
            "xk,kyc->xyc", add_table_x, stacked, preferred_element_type=jnp.float32
        )
        linear = jnp.dot(
            current.reshape(rows_here * cols_here, channels),
            pointwise[level],
            preferred_element_type=jnp.float32,
        ).reshape(rows_here, cols_here, channels)
        mixed = spatial * scale_inv + linear + bias[level]
        state = jax.nn.gelu(mixed, approximate=False).astype(jnp.bfloat16)
    return state[None]


def solution(mesh):
    in_specs = (
        P("mem", "gx", "gy", None),
        P(None, ("gx", "gy"), None, None, "mem", None),
        P(),
        P(),
    )
    out_specs = P("mem", "gx", "gy", None)
    return jax.shard_map(local, mesh=mesh, in_specs=in_specs, out_specs=out_specs, check_vma=False)
```

profile of v0, /device:TPU:33, one launch (start us, length us, event | category | flops | bytes accessed | tf_op | source)
XLA Modules:
  0.0 311.7 jit_solution(10618516805794953704)
XLA Ops:
  9.0 5.1 %fusion.44 = bf16[64,128,128]{2,0,1:T(8,128)(2,1)S(1)} fusion(bf16[128,128,128]{2,1,0:T(8,128)(2,1)} %bitcast.145, bf16[32,128]{1,0:T(8,128)(2,1)S(1)} %fusion.119, bf16[32,128]{1,0:T(8,128)(2,1)S(1)} %cosine_convert_fusion.1), kind=kOutput, calls=%fused_computation.89 | convolution fusion | flops 269516800 | bytes 6307840 | tf_op jit(solution)/shard_map/kx,xyc->kyc/dot_general | solution.py:110
  16.5 8.9 %all-to-all-start = ((bf16[16,2,2,32,128]{4,3,2,1,0:T(8,128)(2,1)}), bf16[16,2,2,32,128]{4,3,2,1,0:T(8,128)(2,1)S(1)}, u32[]{:S(2)}, u32[]{:S(2)}) async-start(bf16[16,2,2,32,128]{4,3,2,1,0:T(8,128)(2,1)} %bitcast.5), calls=%async_computation | async-start | bytes 1048576 | tf_op jit(solution)/shard_map/all_to_all | solution.py:23
  26.1 15.5 %all-to-all-done = bf16[16,2,2,32,128]{4,3,2,1,0:T(8,128)(2,1)S(1)} async-done(((bf16[16,2,2,32,128]{4,3,2,1,0:T(8,128)(2,1)}), bf16[16,2,2,32,128]{4,3,2,1,0:T(8,128)(2,1)S(1)}, u32[]{:S(2)}, u32[]{:S(2)}) %all-to-all-start) | async-done | bytes 524320 | tf_op jit(solution)/shard_map/all_to_all | solution.py:23
  41.7 31.2 %all-gather.7.cloned.1.call-done = bf16[1,2,2,32,128,128]{5,4,3,2,1,0:T(8,128)(2,1)} async-done(((bf16[1,2,2,32,8,128]{5,4,3,2,1,0:T(8,128)(2,1)}), bf16[1,2,2,32,128,128]{5,4,3,2,1,0:T(8,128)(2,1)}) %all-gather.7.cloned.1.call-update) | async-done | bytes 4194320 | tf_op jit(solution)/shard_map/all_gather | solution.py:130
  82.8 9.8 %all-to-all-start.1 = ((bf16[16,2,2,32,128]{4,3,2,1,0:T(8,128)(2,1)}), bf16[16,2,2,32,128]{4,3,2,1,0:T(8,128)(2,1)S(1)}, u32[]{:S(2)}, u32[]{:S(2)}) async-start(bf16[16,2,2,32,128]{4,3,2,1,0:T(8,128)(2,1)} %broadcast_in_dim.18), calls=%async_computation.1 | async-start | bytes 1048576 | tf_op jit(solution)/shard_map/all_to_all | solution.py:29
  92.6 13.7 %fusion.31 = f32[128,128,128]{2,0,1:T(8,128)} fusion(bf16[128,128,128]{2,1,0:T(8,128)(2,1)} %bitcast.146, bf16[3,128,128]{2,1,0:T(8,128)(2,1)S(1)} %copy-done.5), kind=kOutput, calls=%fused_computation.61 | convolution fusion | flops 536870912 | bytes 12615680 | tf_op jit(solution)/shard_map/dot_general | solution.py:144
  106.4 2.2 all-to-all-done.1
  109.7 2.3 copy-done.3
  112.0 23.8 %fusion.2 = bf16[128,128,128]{2,0,1:T(8,128)(2,1)S(1)} fusion(f32[128,128,128]{2,0,1:T(8,128)S(1)} %copy-done.3, f32[128]{0:T(128)S(1)} %get-tuple-element.27, bf16[64,128,128]{2,1,0:T(8,128)(2,1)S(1)} %pad_maximum_fusion.1, bf16[32,128]{1,0:T(8,128)(2,1)S(1)} %fusion.119, bf16[32,128]{1,0:T(8,128)(2,1)S(1)} %cosine_convert_fusion.1), kind=kOutput, calls=%fused_computation.5 | convolution fusion | flops 411074560 | bytes 14696960 | tf_op jit(solution)/shard_map/xk,kyc->xyc/dot_general | solution.py:141
  139.9 21.0 %all_to_all.30 = bf16[16,2,2,32,128]{4,3,2,1,0:T(8,128)(2,1)S(1)} all-to-all(bf16[16,2,2,32,128]{4,3,2,1,0:T(8,128)(2,1)S(1)} %bitcast.151), channel_id=1, replica_groups=mesh['mem'=16,'gx'=4,'gy'=4] {'gx','gy'}, dimensions={0} | all-to-all | bytes 1048576 | tf_op jit(solution)/shard_map/all_to_all | solution.py:23
  163.3 2.2 fusion.51
  171.0 4.0 %all-to-all-start.3 = ((bf16[16,2,2,32,128]{4,3,2,1,0:T(8,128)(2,1)}), bf16[16,2,2,32,128]{4,3,2,1,0:T(8,128)(2,1)S(1)}, u32[]{:S(2)}, u32[]{:S(2)}) async-start(bf16[16,2,2,32,128]{4,3,2,1,0:T(8,128)(2,1)} %broadcast_in_dim.19), calls=%async_computation.3 | async-start | bytes 1048576 | tf_op jit(solution)/shard_map/all_to_all | solution.py:29
  175.7 6.7 %fusion.79 = f32[128,128,128]{2,0,1:T(8,128)} fusion(bf16[128,128,128]{2,0,1:T(8,128)(2,1)} %copy-done, bf16[3,128,128]{2,1,0:T(8,128)(2,1)S(1)} %copy-done.5), kind=kOutput, calls=%fused_computation.117 | convolution fusion | flops 536870912 | bytes 12615680 | tf_op jit(solution)/shard_map/dot_general | solution.py:144
  182.4 8.8 %all-to-all-done.3 = bf16[16,2,2,32,128]{4,3,2,1,0:T(8,128)(2,1)S(1)} async-done(((bf16[16,2,2,32,128]{4,3,2,1,0:T(8,128)(2,1)}), bf16[16,2,2,32,128]{4,3,2,1,0:T(8,128)(2,1)S(1)}, u32[]{:S(2)}, u32[]{:S(2)}) %all-to-all-start.3) | async-done | bytes 524320 | tf_op jit(solution)/shard_map/all_to_all | solution.py:29
  192.3 2.3 copy-done.4
  194.6 23.8 %fusion.5 = bf16[128,128,128]{2,0,1:T(8,128)(2,1)S(1)} fusion(f32[128,128,128]{2,0,1:T(8,128)S(1)} %copy-done.4, f32[128]{0:T(128)S(1)} %get-tuple-element.26, bf16[64,128,128]{2,1,0:T(8,128)(2,1)S(1)} %pad_maximum_fusion.3, bf16[32,128]{1,0:T(8,128)(2,1)S(1)} %fusion.119, bf16[32,128]{1,0:T(8,128)(2,1)S(1)} %cosine_convert_fusion.1), kind=kOutput, calls=%fused_computation.8 | convolution fusion | flops 411074560 | bytes 14696960 | tf_op jit(solution)/shard_map/xk,kyc->xyc/dot_general | solution.py:141
  222.5 20.1 %all_to_all.31 = bf16[16,2,2,32,128]{4,3,2,1,0:T(8,128)(2,1)S(1)} all-to-all(bf16[16,2,2,32,128]{4,3,2,1,0:T(8,128)(2,1)S(1)} %bitcast.150), channel_id=1, replica_groups=mesh['mem'=16,'gx'=4,'gy'=4] {'gx','gy'}, dimensions={0} | all-to-all | bytes 1048576 | tf_op jit(solution)/shard_map/all_to_all | solution.py:23
  245.0 2.2 fusion.55
  252.8 4.3 %all-to-all-start.5 = ((bf16[16,2,2,32,128]{4,3,2,1,0:T(8,128)(2,1)}), bf16[16,2,2,32,128]{4,3,2,1,0:T(8,128)(2,1)S(1)}, u32[]{:S(2)}, u32[]{:S(2)}) async-start(bf16[16,2,2,32,128]{4,3,2,1,0:T(8,128)(2,1)} %broadcast_in_dim.20), calls=%async_computation.5 | async-start | bytes 1048576 | tf_op jit(solution)/shard_map/all_to_all | solution.py:29
  257.1 6.7 %fusion.77 = f32[128,128,128]{2,0,1:T(8,128)} fusion(bf16[128,128,128]{2,0,1:T(8,128)(2,1)} %copy-done.1, bf16[3,128,128]{2,1,0:T(8,128)(2,1)S(1)} %copy-done.5), kind=kOutput, calls=%fused_computation.115 | convolution fusion | flops 536870912 | bytes 12615680 | tf_op jit(solution)/shard_map/dot_general | solution.py:144
  263.8 9.4 %all-to-all-done.5 = bf16[16,2,2,32,128]{4,3,2,1,0:T(8,128)(2,1)S(1)} async-done(((bf16[16,2,2,32,128]{4,3,2,1,0:T(8,128)(2,1)}), bf16[16,2,2,32,128]{4,3,2,1,0:T(8,128)(2,1)S(1)}, u32[]{:S(2)}, u32[]{:S(2)}) %all-to-all-start.5) | async-done | bytes 524320 | tf_op jit(solution)/shard_map/all_to_all | solution.py:29
  274.3 2.3 copy-done.2
  276.6 23.6 %fusion.30 = bf16[1,128,128,128]{3,1,2,0:T(8,128)(2,1)S(1)} fusion(f32[128]{0:T(128)S(1)} %get-tuple-element.28, f32[128,128,128]{2,0,1:T(8,128)S(1)} %copy-done.2, bf16[64,128,128]{2,1,0:T(8,128)(2,1)S(1)} %pad_maximum_fusion.5, bf16[32,128]{1,0:T(8,128)(2,1)S(1)} %fusion.119, bf16[32,128]{1,0:T(8,128)(2,1)S(1)} %cosine_convert_fusion.1), kind=kOutput, calls=%fused_computation.60 | convolution fusion | flops 411074560 | bytes 14696960 | tf_op jit(solution)/shard_map/xk,kyc->xyc/dot_general | solution.py:141
  300.2 4.7 %copy.17 = bf16[1,128,128,128]{3,2,1,0:T(8,128)(2,1)} copy(bf16[1,128,128,128]{3,1,2,0:T(8,128)(2,1)S(1)} %fusion.30) | data formatting | bytes 8388608 | tf_op jit(solution)/shard_map/broadcast_in_dim | solution.py:151
  (77 shorter events, 43.3 us)
Async XLA Ops:
  6.5 66.3 %all-gather.7.cloned.1.call-start = ((), (), s32[]{:S(2)}) async-start(), calls=%async_computation.6 | async-start | bytes 4456448 | tf_op jit(solution)/shard_map/all_gather | solution.py:130
  14.7 77.9 %copy-start.6 = (f32[3,128]{1,0:T(4,128)S(1)}, f32[3,128]{1,0:T(4,128)}, u32[]{:S(2)}) copy-start(f32[3,128]{1,0:T(4,128)} %param.7) | copy-start | bytes 4612
  14.7 78.0 %copy-start.5 = (bf16[3,128,128]{2,1,0:T(8,128)(2,1)S(1)}, bf16[3,128,128]{2,1,0:T(8,128)(2,1)}, u32[]{:S(2)}) copy-start(bf16[3,128,128]{2,1,0:T(8,128)(2,1)} %param.6) | copy-start | bytes 294916
  16.5 25.1 %all-to-all-start = ((bf16[16,2,2,32,128]{4,3,2,1,0:T(8,128)(2,1)}), bf16[16,2,2,32,128]{4,3,2,1,0:T(8,128)(2,1)S(1)}, u32[]{:S(2)}, u32[]{:S(2)}) async-start(bf16[16,2,2,32,128]{4,3,2,1,0:T(8,128)(2,1)} %bitcast.5), calls=%async_computation | async-start | bytes 1048576 | tf_op jit(solution)/shard_map/all_to_all | solution.py:23
  25.3 135.7 %all-gather.9.cloned.1.call-start = ((), (), s32[]{:S(2)}) async-start(), calls=%async_computation.7 | async-start | bytes 4456448 | tf_op jit(solution)/shard_map/all_gather | solution.py:130
  82.8 25.9 %all-to-all-start.1 = ((bf16[16,2,2,32,128]{4,3,2,1,0:T(8,128)(2,1)}), bf16[16,2,2,32,128]{4,3,2,1,0:T(8,128)(2,1)S(1)}, u32[]{:S(2)}, u32[]{:S(2)}) async-start(bf16[16,2,2,32,128]{4,3,2,1,0:T(8,128)(2,1)} %broadcast_in_dim.18), calls=%async_computation.1 | async-start | bytes 1048576 | tf_op jit(solution)/shard_map/all_to_all | solution.py:29
  108.6 3.4 %copy-start.3 = (f32[128,128,128]{2,0,1:T(8,128)S(1)}, f32[128,128,128]{2,0,1:T(8,128)}, u32[]{:S(2)}) copy-start(f32[128,128,128]{2,0,1:T(8,128)} %fusion.31) | copy-start | bytes 25165828
  135.8 2.0 copy-start
  171.0 20.2 %all-to-all-start.3 = ((bf16[16,2,2,32,128]{4,3,2,1,0:T(8,128)(2,1)}), bf16[16,2,2,32,128]{4,3,2,1,0:T(8,128)(2,1)S(1)}, u32[]{:S(2)}, u32[]{:S(2)}) async-start(bf16[16,2,2,32,128]{4,3,2,1,0:T(8,128)(2,1)} %broadcast_in_dim.19), calls=%async_computation.3 | async-start | bytes 1048576 | tf_op jit(solution)/shard_map/all_to_all | solution.py:29
  175.0 67.8 %all-gather.11.cloned.1.call-start = ((), (), s32[]{:S(2)}) async-start(), calls=%async_computation.8 | async-start | bytes 4456448 | tf_op jit(solution)/shard_map/all_gather | solution.py:130
  191.2 3.4 %copy-start.4 = (f32[128,128,128]{2,0,1:T(8,128)S(1)}, f32[128,128,128]{2,0,1:T(8,128)}, u32[]{:S(2)}) copy-start(f32[128,128,128]{2,0,1:T(8,128)} %fusion.79) | copy-start | bytes 25165828
  218.4 2.0 copy-start.1
  252.8 20.4 %all-to-all-start.5 = ((bf16[16,2,2,32,128]{4,3,2,1,0:T(8,128)(2,1)}), bf16[16,2,2,32,128]{4,3,2,1,0:T(8,128)(2,1)S(1)}, u32[]{:S(2)}, u32[]{:S(2)}) async-start(bf16[16,2,2,32,128]{4,3,2,1,0:T(8,128)(2,1)} %broadcast_in_dim.20), calls=%async_computation.5 | async-start | bytes 1048576 | tf_op jit(solution)/shard_map/all_to_all | solution.py:29
  273.2 3.4 %copy-start.2 = (f32[128,128,128]{2,0,1:T(8,128)S(1)}, f32[128,128,128]{2,0,1:T(8,128)}, u32[]{:S(2)}) copy-start(f32[128,128,128]{2,0,1:T(8,128)} %fusion.77) | copy-start | bytes 25165828
Sparse Core Ops, SparseCore 0:
  9.7 63.0 all-gather.6
  75.2 61.2 all-gather.8
  178.2 59.3 all-gather.10
where the time goes:
time: 318 us; the launch traced here: 312 us
  matrix products  137 us (43%)
  waiting for transfers between devices  68.5 us (22%)
  blocking collectives  41.1 us (13%)
  starting transfers between devices  27 us (8%)
  local copies, waits for them, and re-layouts  22.2 us (7%)
  between operations  13.8 us (4%)
    dot_general x3, matrix products, local(): jnp.einsum('xk,kyc->xyc', add_table_x, stacked, preferred_element_type=jn...  71.2 us
    all_to_all x2, blocking collectives, sent_and_summed(): lax.all_to_all(blocks, axis, split_axis=0, concat_axis=0, tiled=True)  41.1 us
    all_gather x3, waiting for transfers between devices, local(): lax.all_gather(weights_here, 'mem', axis=3, tiled=True)  31.2 us
    dot_general x3, matrix products, local(): jnp.dot(current.reshape(rows_here * cols_here, channels), pointwise[level...  27.2 us
    all_to_all x3, waiting for transfers between devices, from_everyone(): return lax.all_to_all(copies, axis, split_axis=0, concat_axis=0, tiled=True)  20.5 us
    all_to_all x3, starting transfers between devices, from_everyone(): return lax.all_to_all(copies, axis, split_axis=0, concat_axis=0, tiled=True)  18 us
    all_to_all x1, waiting for transfers between devices, sent_and_summed(): lax.all_to_all(blocks, axis, split_axis=0, concat_axis=0, tiled=True)  15.5 us
    unnamed x14, local copies, waits for them, and re-layouts  11 us
  transfers between devices with their start and end apart: 7, of which 5 were waited for; matrix products, arithmetic and copies ran while one was open for 32% of the time, Pallas kernels for 0%

commit v1 on v0

v1 whole, which is shorter than its diff:
```python
import math

import jax
import jax.numpy as jnp
from jax import lax
from jax.experimental import pallas as pl
from jax.experimental.pallas import tpu as pltpu
from jax.sharding import PartitionSpec as P


KX = 32
KY = 32
NX = 512
NY = 512
LAYERS = 3
GRID = ("gx", "gy")
ZN = 8
RC = 4 * KY
SC = RC + 4
SG = 2 * KY + 4


def grid_index(z, core):
    return ((z // 4) * 2 + core) * 4 + z % 4


PAIR = [(grid_index(z, c), grid_index(z, 1 - c)) for z in range(ZN) for c in range(2)]
LINES = [[grid_index(z, c) for z in range(ZN)] for c in range(2)]


def angle_tables(rows_here, cols_here):
    gx = lax.axis_index("gx")
    gy = lax.axis_index("gy")
    row = lax.broadcasted_iota(jnp.int32, (KX + KY, 128), 0)
    lane = lax.broadcasted_iota(jnp.int32, (KX + KY, 128), 1)
    z = row % ZN
    core = (gx + (row // ZN) % 2) % 2
    index_x = 2 * (((z // 4) * 2 + core) * 4 + z % 4) + row // (2 * ZN)
    freq_x = jnp.where(index_x < KX // 2, index_x, NX - KX + index_x)
    in_x = row < KX
    freq = jnp.where(in_x, freq_x, row - KX)
    position = lane + jnp.where(in_x, gx * rows_here, gy * cols_here)
    angles = 2.0 * math.pi / NX * (freq * position % NX).astype(jnp.float32)
    return jnp.cos(angles), jnp.sin(angles)


def dot(a, b):
    return jnp.dot(a, b, preferred_element_type=jnp.float32)


GROUP = 8
BLOCK = 16


def copies_in(hbm, buf, sems):
    return [
        pltpu.make_async_copy(hbm.at[pl.ds(n * BLOCK, BLOCK)], buf.at[pl.ds(n * BLOCK, BLOCK)], sems.at[n])
        for n in range(buf.shape[0] // BLOCK)
    ]


def forward_group(i, u_ref, fy, h_ref):
    for e in range(GROUP // 2):
        x = i * GROUP + 2 * e
        h = dot(fy, jnp.concatenate([u_ref[x], u_ref[x + 1]], axis=1))
        h_ref[pl.ds(x, 2 * KY, stride=SC), :] = h[:, :128]
        h_ref[pl.ds(x + 1, 2 * KY, stride=SC), :] = h[:, 128:]


def modes_of(h_ref, m_ref, fx_ref, keep_ref, send_ref):
    fx = fx_ref[...]
    for q in range(0, KY, 2):
        rhs = jnp.concatenate(
            [
                jnp.concatenate(
                    [
                        h_ref[pl.ds((part * KY + q + d) * SC, 128), :].astype(jnp.bfloat16)
                        for part in range(2)
                    ],
                    axis=0,
                )
                for d in range(2)
            ],
            axis=1,
        )
        out = dot(fx, rhs)
        for d in range(2):
            for s in range(4):
                m_ref[pl.ds((q + d) * 4 + s, 16, stride=SC), :] = out[
                    16 * s : 16 * s + 16, 128 * d : 128 * d + 128
                ]
    for k in range(ZN):
        keep_ref[k] = m_ref[pl.ds(k * SC, RC), :]
        send_ref[k] = m_ref[pl.ds((ZN + k) * SC, RC), :].astype(jnp.bfloat16)


def first_kernel(
    u_hbm, cos_ref, sin_ref,
    keep_ref, send_ref, fx_ref, ix_ref, fy_ref, iy_ref,
    u_buf, h_ref, m_ref, sems,
):
    loads = copies_in(u_hbm, u_buf, sems)
    for c in loads:
        c.start()
    cx, cy = cos_ref[:KX], cos_ref[KX:]
    sx, sy = sin_ref[:KX], sin_ref[KX:]
    bf16 = jnp.bfloat16
    left = jnp.concatenate([cx, -sx], axis=0)
    right = jnp.concatenate([sx, cx], axis=0)
    table = jnp.concatenate([left, right], axis=1).astype(bf16)
    fx_ref[...] = (table.astype(jnp.float32) * (1.0 / math.sqrt(NX * NY))).astype(bf16)
    blank = jnp.zeros((128 - 2 * KX, 128), jnp.float32)
    ix_ref[:128] = jnp.concatenate([left, blank], axis=0).T[:, : 2 * KX].astype(bf16)
    ix_ref[128:] = jnp.concatenate([right, blank], axis=0).T[:, : 2 * KX].astype(bf16)
    fy_ref[...] = jnp.concatenate([cy, -sy], axis=0).astype(bf16)
    double = jnp.where(lax.broadcasted_iota(jnp.int32, (KY, 128), 0) == 0, 1.0, 2.0)
    iy_ref[...] = jnp.concatenate([double * cy, -(double * sy), blank], axis=0).T.astype(bf16)
    per = BLOCK // GROUP

    for n, c in enumerate(loads):
        c.wait()

        def step(i, carry):
            forward_group(i, u_buf, fy_ref[...], h_ref)
            return carry

        lax.fori_loop(n * per, (n + 1) * per, step, 0)
    modes_of(h_ref, m_ref, fx_ref, keep_ref, send_ref)


def layer_body(u_hbm, own_ref, oth_ref, ix_ref, iy_ref, w_ref, b_ref, out_hbm, u_buf, bs_ref, g_ref, sems, forward):
    loads = copies_in(u_hbm, u_buf, sems.at[0])
    for c in loads:
        c.start()
    for k in range(ZN):
        bs_ref[pl.ds(k * SC, RC), :] = own_ref[k].astype(jnp.float32)
        bs_ref[pl.ds((ZN + k) * SC, RC), :] = oth_ref[k].astype(jnp.float32)
    scale = 1.0 / math.sqrt(2 * KX * KY)
    ix = ix_ref[...]
    for q in range(0, KY, 2):
        rhs = jnp.concatenate(
            [
                jnp.concatenate(
                    [bs_ref[pl.ds((q + d) * 4 + s, 16, stride=SC), :] for s in range(4)], axis=0
                ).astype(jnp.bfloat16)
                for d in range(2)
            ],
            axis=1,
        )
        for part in range(2):
            g = dot(ix[128 * part : 128 * part + 128], rhs) * scale
            for d in range(2):
                g_ref[pl.ds(part * KY + q + d, 128, stride=SG), :] = g[:, 128 * d : 128 * d + 128]
    for c in loads:
        c.wait()
    steps = u_buf.shape[0] // GROUP

    def store(i):
        return pltpu.make_async_copy(
            u_buf.at[pl.ds(i * GROUP, GROUP)], out_hbm.at[pl.ds(i * GROUP, GROUP)], sems.at[1, i]
        )

    def point(i):
        w = w_ref[...]
        iy = iy_ref[...]
        bias = b_ref[...]
        pad = jnp.zeros((128 - 2 * KY, 128), jnp.bfloat16)
        for e in range(GROUP):
            x = i * GROUP + e
            gx = g_ref[pl.ds(x * SG, 2 * KY), :].astype(jnp.bfloat16)
            lhs = jnp.concatenate([u_buf[x], iy], axis=1)
            rhs = jnp.concatenate([w, gx, pad], axis=0)
            z = dot(lhs, rhs) + bias
            half = 0.5 * z
            u_buf[x] = (half + half * lax.erf(z * math.sqrt(0.5))).astype(jnp.bfloat16)

    def step(i, carry):
        if forward is not None:
            forward(i - 1)
        point(i)
        store(i).start()
        return carry

    point(0)
    store(0).start()
    lax.fori_loop(1, steps, step, 0)
    if forward is not None:
        forward(steps - 1)

    def finish():
        for i in range(steps):
            store(i).wait()

    return finish


def mid_kernel(
    u_hbm, own_ref, oth_ref, ix_ref, iy_ref, w_ref, b_ref, fy_ref, fx_ref,
    out_hbm, keep_ref, send_ref, u_buf, bs_ref, g_ref, h_ref, m_ref, sems,
):
    def forward(i):
        forward_group(i, u_buf, fy_ref[...], h_ref)

    finish = layer_body(
        u_hbm, own_ref, oth_ref, ix_ref, iy_ref, w_ref, b_ref, out_hbm, u_buf, bs_ref, g_ref, sems, forward
    )
    modes_of(h_ref, m_ref, fx_ref, keep_ref, send_ref)
    finish()


def last_kernel(
    u_hbm, own_ref, oth_ref, ix_ref, iy_ref, w_ref, b_ref, out_hbm, u_buf, bs_ref, g_ref, sems
):
    layer_body(
        u_hbm, own_ref, oth_ref, ix_ref, iy_ref, w_ref, b_ref, out_hbm, u_buf, bs_ref, g_ref, sems, None
    )()


def few_kernel(a_ref, w_ref, out_ref, as_ref, bs_ref):
    members = a_ref.shape[0]
    as_ref[...] = a_ref[...].astype(jnp.float32).reshape(members * 8, 128)
    for e in range(2):
        for jj in range(2):
            w = jnp.concatenate(
                [
                    w_ref[:, jj, ri, e].astype(jnp.float32).reshape(128, 128).astype(jnp.bfloat16)
                    for ri in range(2)
                ],
                axis=1,
            )
            row_re = e * 4 + jj
            row_im = e * 4 + 2 + jj
            re = dot(as_ref[pl.ds(row_re, members, stride=8), :].astype(jnp.bfloat16), w)
            im = dot(as_ref[pl.ds(row_im, members, stride=8), :].astype(jnp.bfloat16), w)
            bs_ref[pl.ds(row_re, members, stride=8), :] = re[:, :128] - im[:, 128:]
            bs_ref[pl.ds(row_im, members, stride=8), :] = re[:, 128:] + im[:, :128]
    out_ref[...] = bs_ref[...].reshape(members, 8, 128).astype(jnp.bfloat16)


def many_kernel(s_ref, w_hbm, out_ref, w_buf, sems):
    loads = [
        pltpu.make_async_copy(w_hbm.at[:, :, pl.ds(4 * b, 4)], w_buf.at[b], sems.at[b])
        for b in range(KY // 4)
    ]
    for c in loads:
        c.start()
    a = s_ref[0].astype(jnp.float32)
    for k in range(1, ZN):
        a = a + s_ref[k].astype(jnp.float32)
    row = lax.broadcasted_iota(jnp.int32, (16, 128), 0)
    lower = row % 4 < 2
    blocks = []
    for b in range(KY // 4):
        rows = a[16 * b : 16 * b + 16]
        acc = None
        loads[b].wait()
        for dq in range(4):
            for jj in range(2):
                mine = (row == dq * 4 + jj) | (row == dq * 4 + 2 + jj)
                lhs = jnp.where(mine, rows, 0.0).astype(jnp.bfloat16)
                w = jnp.concatenate([w_buf[b, jj, 0, dq], w_buf[b, jj, 1, dq]], axis=1)
                part = dot(lhs, w)
                acc = part if acc is None else acc + part
        straight = acc[:, :128]
        cross = acc[:, 128:]
        up = jnp.concatenate([cross[2:], cross[:2]], axis=0)
        down = jnp.concatenate([cross[14:], cross[:14]], axis=0)
        blocks.append(jnp.where(lower, straight - up, straight + down).astype(jnp.bfloat16))
    full = jnp.concatenate(blocks, axis=0)
    for k in range(ZN):
        out_ref[k] = full


V = pl.BlockSpec(memory_space=pltpu.VMEM)
H = pl.BlockSpec(memory_space=pltpu.HBM)


def call(kernel, args, outs, scratch=(), in_hbm=(), out_hbm=(), alias=None, limit=24):
    args = [
        pltpu.with_memory_space_constraint(a, pltpu.HBM) if i in in_hbm else a for i, a in enumerate(args)
    ]
    outs = [pltpu.HBM(o.shape, o.dtype) if i in out_hbm else o for i, o in enumerate(outs)]
    return pl.pallas_call(
        kernel,
        out_shape=outs,
        in_specs=[H if i in in_hbm else V for i in range(len(args))],
        out_specs=[H if i in out_hbm else V for i in range(len(outs))],
        scratch_shapes=list(scratch),
        input_output_aliases=alias or {},
        compiler_params=pltpu.CompilerParams(vmem_limit_bytes=limit << 20),
    )(*args)


def local(field, spectral, pointwise, bias):
    u = field[0]
    rows_here, cols_here, channels = u.shape
    members = lax.axis_size("mem")
    bf16, f32 = jnp.bfloat16, jnp.float32
    sds = jax.ShapeDtypeStruct
    dma = pltpu.SemaphoreType.DMA
    chunks = [sds((ZN, RC, channels), f32), sds((ZN, RC, channels), bf16)]
    ub = pltpu.VMEM(u.shape, bf16)
    bs = pltpu.VMEM((2 * ZN * SC, channels), f32)
    gs = pltpu.VMEM((rows_here * SG, channels), f32)
    hs = pltpu.VMEM((2 * KY * SC, channels), f32)
    blocks, steps = rows_here // BLOCK, rows_here // GROUP

    weights = {
        level: lax.all_gather(spectral[level], "mem", axis=3, tiled=True) for level in range(1, LAYERS)
    }
    first = spectral[0].reshape(2, 2, members, 2, 8, channels)
    first = jnp.moveaxis(first, 2, 0)
    first = lax.all_to_all(first, "mem", 0, 0, tiled=True)

    cosines, sines = angle_tables(rows_here, cols_here)
    keep, send, forward_x, inverse_x, forward_y, inverse_y = call(
        first_kernel,
        (u, cosines, sines),
        [
            *chunks,
            sds((2 * KX, 2 * rows_here), bf16),
            sds((2 * rows_here, 2 * KX), bf16),
            sds((2 * KY, cols_here), bf16),
            sds((cols_here, 128), bf16),
        ],
        (ub, hs, bs, dma((blocks,))),
        in_hbm=(0,),
    )
    for level in range(LAYERS):
        other = lax.ppermute(send, GRID, PAIR)
        paired = (keep + other.astype(f32)).astype(bf16)
        if level == 0:
            paired, first = lax.optimization_barrier((paired, first))
        parts = lax.all_to_all(paired, GRID, 0, 0, axis_index_groups=LINES, tiled=True)
        if level == 0:
            coeffs = parts.astype(f32).sum(axis=0).astype(bf16).reshape(members, 8, channels)
            coeffs = lax.all_to_all(coeffs, "mem", 0, 0, tiled=True)
            small = pltpu.VMEM((members * 8, channels), f32)
            (mixed,) = call(few_kernel, (coeffs, first), [sds((members, 8, channels), bf16)], (small, small))
            mixed = lax.all_to_all(mixed, "mem", 0, 0, tiled=True).reshape(RC, channels)
            mixed = jnp.broadcast_to(mixed, (ZN, RC, channels))
        else:
            (mixed,) = call(
                many_kernel,
                (parts, weights[level]),
                [sds((ZN, RC, channels), bf16)],
                (pltpu.VMEM((KY // 4, 2, 2, 4, channels, channels), bf16), dma((KY // 4,))),
                in_hbm=(1,),
            )
        own = lax.all_to_all(mixed, GRID, 0, 0, axis_index_groups=LINES, tiled=True)
        oth = lax.ppermute(own, GRID, PAIR)
        args = (u, own, oth, inverse_x, inverse_y, pointwise[level], bias[level][None])
        if level < LAYERS - 1:
            u, keep, send = call(
                mid_kernel,
                (*args, forward_y, forward_x),
                [sds(u.shape, bf16), *chunks],
                (ub, bs, gs, hs, bs, dma((2, steps))),
                in_hbm=(0,),
                out_hbm=(0,),
            )
        else:
            (u,) = call(
                last_kernel, args, [sds(u.shape, bf16)], (ub, bs, gs, dma((2, steps))),
                in_hbm=(0,), out_hbm=(0,),
            )
    return u[None]


def solution(mesh):
    in_specs = (
        P("mem", "gx", "gy", None),
        P(None, ("gx", "gy"), None, None, "mem", None),
        P(),
        P(),
    )
    out_specs = P("mem", "gx", "gy", None)
    return jax.shard_map(local, mesh=mesh, in_specs=in_specs, out_specs=out_specs, check_vma=False)
```

time: 318 us -> 198 us (0.62); the launches traced: 312 us -> 195 us
  matrix products: 137 us -> 0 us
  blocking collectives: 41.1 us -> 88.9 us
  waiting for transfers between devices: 68.5 us -> 23.9 us
  Pallas kernels: 0 us -> 38.6 us
  local copies, waits for them, and re-layouts: 22.2 us -> 2.81 us
    dot_general x27 -> x0, matrix products: 137 us -> none  [the longest x3 71.2 us: local(): jnp.einsum('xk,kyc->xyc', add_table_x, stacked, preferred_element_type=jn...]
    all_to_all x2 -> x7, blocking collectives: 41.1 us -> 88.9 us  [the longest x3 40.9 us: local(): own = lax.all_to_all(mixed, GRID, 0, 0, axis_index_groups=LINES, tiled=True)]
    pallas_call x0 -> x7, Pallas kernels: none -> 38.6 us  [call(): pl.pallas_call(kernel, out_shape=outs, in_specs=[H if i in in_hbm else V...]
    all_gather x3 -> x2, waiting for transfers between devices: 31.2 us -> 0.01 us  [local(): lax.all_gather(spectral[level], 'mem', axis=3, tiled=True)]
    all_to_all x4 -> x2, waiting for transfers between devices: 35.9 us -> 17.4 us  [the longest x1 9.01 us: local(): lax.all_to_all(paired, GRID, 0, 0, axis_index_groups=LINES, tiled=True)]
    all_to_all x4 -> x2, starting transfers between devices: 26.9 us -> 11.3 us  [the longest x1 6.75 us: local(): first = lax.all_to_all(first, 'mem', 0, 0, tiled=True)]
    ppermute x0 -> x6, starting transfers between devices: none -> 14.9 us  [the longest x3 13.1 us: local(): oth = lax.ppermute(own, GRID, PAIR)]
    unnamed x14 -> x4, local copies, waits for them, and re-layouts: 11 us -> 0.01 us
  transfers between devices with their start and end apart: 7 -> 10, of which waited for: 5 -> 7; matrix products, arithmetic and copies ran while one was open for 32% -> 1% of each run, Pallas kernels for 0% -> 14%
where the time goes in v1:
time: 198 us; the launch traced here: 195 us
  blocking collectives  88.9 us (45%)
  Pallas kernels  38.6 us (19%)
  starting transfers between devices  26.2 us (13%)
  waiting for transfers between devices  23.9 us (12%)
  between operations  13.6 us (7%)
  local copies, waits for them, and re-layouts  2.81 us (1%)
    all_to_all x3, blocking collectives, local(): own = lax.all_to_all(mixed, GRID, 0, 0, axis_index_groups=LINES, tiled=True)  40.9 us
    pallas_call x7, Pallas kernels, call(): pl.pallas_call(kernel, out_shape=outs, in_specs=[H if i in in_hbm else V...  38.6 us
    all_to_all x2, blocking collectives, local(): lax.all_to_all(paired, GRID, 0, 0, axis_index_groups=LINES, tiled=True)  29.3 us
    ppermute x3, starting transfers between devices, local(): oth = lax.ppermute(own, GRID, PAIR)  13.1 us
    all_to_all x1, blocking collectives, local(): mixed = lax.all_to_all(mixed, 'mem', 0, 0, tiled=True).reshape(RC, channels)  9.5 us
    all_to_all x1, blocking collectives, local(): coeffs = lax.all_to_all(coeffs, 'mem', 0, 0, tiled=True)  9.2 us
    all_to_all x1, waiting for transfers between devices, local(): lax.all_to_all(paired, GRID, 0, 0, axis_index_groups=LINES, tiled=True)  9.01 us
    all_to_all x1, waiting for transfers between devices, local(): first = lax.all_to_all(first, 'mem', 0, 0, tiled=True)  8.41 us
  transfers between devices with their start and end apart: 10, of which 7 were waited for; matrix products, arithmetic and copies ran while one was open for 1% of the time, Pallas kernels for 14%

profile of v1, /device:TPU:33, one launch (start us, length us, event | category | flops | bytes accessed | tf_op | source)
XLA Modules:
  0.0 195.3 jit_solution(10657467847397201212)
XLA Ops:
  6.5 2.0 %fusion.18 = (bf16[1,2,2,32,8,128]{5,4,3,2,1,0:T(8,128)(2,1)}, bf16[1,2,2,32,8,128]{5,4,3,2,1,0:T(8,128)(2,1)S(1)}, bf16[1,2,2,32,8,128]{5,4,3,2,1,0:T(8,128)(2,1)}) fusion(bf16[3,2,2,32,8,128]{5,4,3,2,1,0:T(8,128)(2,1)} %param.5), kind=kLoop, calls=%fused_computation.59 | loop fusion | bytes 1572864 | tf_op jit(solution)/shard_map/slice | solution.py:309
  9.8 4.5 %shard_map.46 = (f32[8,128,128]{2,1,0:T(8,128)S(1)}, bf16[8,128,128]{2,1,0:T(8,128)(2,1)S(1)}, bf16[64,256]{1,0:T(8,128)(2,1)S(1)}, bf16[256,64]{1,0:T(8,128)(2,...) custom-call(bf16[128,128,128]{2,1,0:T(8,128)(2,1)} %bitcast.16, ...), custom_call_target="tpu_custom_call" | custom-call | tf_op jit(solution)/shard_map/pallas_call | solution.py:283
  15.8 6.8 %all-to-all-start = ((bf16[16,2,2,2,8,128]{5,4,3,2,1,0:T(8,128)(2,1)}), bf16[16,2,2,2,8,128]{5,4,3,2,1,0:T(8,128)(2,1)S(1)}, u32[]{:S(2)}, u32[]{:S(2)}) async-start(bf16[16,2,2,2,8,128]{5,4,3,2,1,0:T(8,128)(2,1)} %bitcast.15), calls=%async_computation | async-start | bytes 524288 | tf_op jit(solution)/shard_map/all_to_all | solution.py:313
  22.6 8.4 %all-to-all-done.w_ref = bf16[16,2,2,2,8,128]{5,4,3,2,1,0:T(8,128)(2,1)S(1)} async-done(((bf16[16,2,2,2,8,128]{5,4,3,2,1,0:T(8,128)(2,1)}), bf16[16,2,2,2,8,128]{5,4,3,2,1,0:T(8,128)(2,1)S(1)}, u32[]{:S(2)}, u32[]{:S(2)}) %all-to-all-start) | async-done | bytes 262176 | tf_op jit(solution)/shard_map/all_to_all | solution.py:313
  31.0 16.5 %all_to_all.45 = bf16[8,128,128]{2,1,0:T(8,128)(2,1)S(1)} all-to-all(bf16[8,128,128]{2,1,0:T(8,128)(2,1)S(1)} %add_convert_fusion.2), channel_id=1, replica_groups={{0,1,2,3,8,9,10,11},{4,5,6,7,12,13,14,15},{16,17,18,19,24,25,26,27},{20..., dimensions={0} | all-to-all | bytes 524288 | tf_op jit(solution)/shard_map/all_to_all | solution.py:334
  47.6 9.2 %all_to_all.46.a_ref = bf16[16,8,128]{2,1,0:T(8,128)(2,1)S(1)} all-to-all(bf16[16,8,128]{2,1,0:T(8,128)(2,1)S(1)} %bitcast.21), channel_id=1, replica_groups=mesh['mem'=16,'gx'=4,'gy'=4] {'mem'}, dimensions={0} | all-to-all | bytes 65536 | tf_op jit(solution)/shard_map/all_to_all | solution.py:337
  57.0 9.5 %all_to_all.47 = bf16[16,8,128]{2,1,0:T(8,128)(2,1)S(1)} all-to-all(bf16[16,8,128]{2,1,0:T(8,128)(2,1)S(1)} %shard_map.47), channel_id=1, replica_groups=mesh['mem'=16,'gx'=4,'gy'=4] {'mem'}, dimensions={0} | all-to-all | bytes 65536 | tf_op jit(solution)/shard_map/all_to_all | solution.py:340
  66.5 12.0 %all_to_all.48.own_ref = bf16[8,128,128]{2,1,0:T(8,128)(2,1)S(1)} all-to-all(bf16[8,128,128]{2,1,0:T(8,128)(2,1)S(1)} %broadcast_in_dim.16), channel_id=1, replica_groups={{0,1,2,3,8,9,10,11},{4,5,6,7,12,13,14,15},{16,17,18,19,24,25,26,27},{20..., dimensions={0} | all-to-all | bytes 524288 | tf_op jit(solution)/shard_map/all_to_all | solution.py:350
  78.5 7.3 %collective-permute-start.1 = (bf16[8,128,128]{2,1,0:T(8,128)(2,1)S(1)}, bf16[8,128,128]{2,1,0:T(8,128)(2,1)S(1)}, u32[]{:S(2)}, u32[]{:S(2)}) collective-permute-start(bf16[8,128,128]{2,1,0:T(8,128)(2,1)S(1)} %all_to_all.48.own_ref), channel_id=1, source_target_pairs={{0,4},{4,0},{1,5},{5,1},{2,6},{6,2},{3,7},{7,3},{8,12},{12,8},{9,1... | collective-permute-start | bytes 786440 | tf_op jit(solution)/shard_map/ppermute | solution.py:351
  87.0 9.5 %shard_map.48 = (bf16[128,128,128]{2,1,0:T(8,128)(2,1)}, f32[8,128,128]{2,1,0:T(8,128)S(1)}, bf16[8,128,128]{2,1,0:T(8,128)(2,1)S(1)}) custom-call(bf16[128,128,128]{2,1,0:T(8,128)(2,1)} %bitcast.17, bf16[8,128,128]{2,1,0:T(8,128)(2,1)S(1)} %all_to_all.48.own_ref, bf16[8,128,128]{2,1,0:T(8,128)(2,1)S(1)} %collective-permute-done.1.oth_ref, ...), custom_call_target="tpu_custom_call" | custom-call | tf_op jit(solution)/shard_map/pallas_call | solution.py:283
  97.0 1.2 collective-permute-done.2
  98.2 12.7 %all_to_all.49.s_ref = bf16[8,128,128]{2,1,0:T(8,128)(2,1)S(1)} all-to-all(bf16[8,128,128]{2,1,0:T(8,128)(2,1)S(1)} %add_convert_fusion.1), channel_id=1, replica_groups={{0,1,2,3,8,9,10,11},{4,5,6,7,12,13,14,15},{16,17,18,19,24,25,26,27},{20..., dimensions={0} | all-to-all | bytes 524288 | tf_op jit(solution)/shard_map/all_to_all | solution.py:334
  110.9 3.1 %shard_map.49 = bf16[8,128,128]{2,1,0:T(8,128)(2,1)S(1)} custom-call(bf16[8,128,128]{2,1,0:T(8,128)(2,1)S(1)} %all_to_all.49.s_ref, bf16[2,2,32,128,128]{4,3,2,1,0:T(8,128)(2,1)} %bitcast.19), custom_call_target="tpu_custom_call" | custom-call | tf_op jit(solution)/shard_map/pallas_call | solution.py:283
  114.1 14.5 %all_to_all.50.own_ref = bf16[8,128,128]{2,1,0:T(8,128)(2,1)S(1)} all-to-all(bf16[8,128,128]{2,1,0:T(8,128)(2,1)S(1)} %shard_map.49), channel_id=1, replica_groups={{0,1,2,3,8,9,10,11},{4,5,6,7,12,13,14,15},{16,17,18,19,24,25,26,27},{20..., dimensions={0} | all-to-all | bytes 524288 | tf_op jit(solution)/shard_map/all_to_all | solution.py:350
  128.6 2.9 %collective-permute-start.3 = (bf16[8,128,128]{2,1,0:T(8,128)(2,1)S(1)}, bf16[8,128,128]{2,1,0:T(8,128)(2,1)S(1)}, u32[]{:S(2)}, u32[]{:S(2)}) collective-permute-start(bf16[8,128,128]{2,1,0:T(8,128)(2,1)S(1)} %all_to_all.50.own_ref), channel_id=1, source_target_pairs={{0,4},{4,0},{1,5},{5,1},{2,6},{6,2},{3,7},{7,3},{8,12},{12,8},{9,1... | collective-permute-start | bytes 786440 | tf_op jit(solution)/shard_map/ppermute | solution.py:351
  131.5 1.2 collective-permute-done.3.oth_ref
  132.6 9.5 %shard_map.50 = (bf16[128,128,128]{2,1,0:T(8,128)(2,1)}, f32[8,128,128]{2,1,0:T(8,128)S(1)}, bf16[8,128,128]{2,1,0:T(8,128)(2,1)S(1)}) custom-call(bf16[128,128,128]{2,1,0:T(8,128)(2,1)} %get-tuple-element.27.u_hbm, bf16[8,128,128]{2,1,0:T(8,128)(2,1)S(1)} %all_to_all.50.own_ref, bf16[8,128,128]{2,1,0:T(8,128)(2,1)S(1)} %collective-permute-done.3.oth_ref, ...), custom_call_target="tpu_custom_call" | custom-call | tf_op jit(solution)/shard_map/pallas_call | solution.py:283
  142.7 1.2 collective-permute-done.4
  144.6 4.6 %all-to-all-start.7 = ((bf16[8,128,128]{2,1,0:T(8,128)(2,1)}), bf16[8,128,128]{2,1,0:T(8,128)(2,1)S(1)}, u32[]{:S(2)}, u32[]{:S(2)}) async-start(bf16[8,128,128]{2,1,0:T(8,128)(2,1)} %add_convert_fusion), calls=%async_computation.7 | async-start | bytes 524288 | tf_op jit(solution)/shard_map/all_to_all | solution.py:334
  149.2 9.0 %all-to-all-done.7.s_ref = bf16[8,128,128]{2,1,0:T(8,128)(2,1)S(1)} async-done(((bf16[8,128,128]{2,1,0:T(8,128)(2,1)}), bf16[8,128,128]{2,1,0:T(8,128)(2,1)S(1)}, u32[]{:S(2)}, u32[]{:S(2)}) %all-to-all-start.7) | async-done | bytes 262176 | tf_op jit(solution)/shard_map/all_to_all | solution.py:334
  158.2 3.1 %shard_map.51 = bf16[8,128,128]{2,1,0:T(8,128)(2,1)S(1)} custom-call(bf16[8,128,128]{2,1,0:T(8,128)(2,1)S(1)} %all-to-all-done.7.s_ref, bf16[2,2,32,128,128]{4,3,2,1,0:T(8,128)(2,1)} %bitcast.18), custom_call_target="tpu_custom_call" | custom-call | tf_op jit(solution)/shard_map/pallas_call | solution.py:283
  161.3 14.5 %all_to_all.51.own_ref = bf16[8,128,128]{2,1,0:T(8,128)(2,1)S(1)} all-to-all(bf16[8,128,128]{2,1,0:T(8,128)(2,1)S(1)} %shard_map.51), channel_id=1, replica_groups={{0,1,2,3,8,9,10,11},{4,5,6,7,12,13,14,15},{16,17,18,19,24,25,26,27},{20..., dimensions={0} | all-to-all | bytes 524288 | tf_op jit(solution)/shard_map/all_to_all | solution.py:350
  175.8 2.9 %collective-permute-start.5 = (bf16[8,128,128]{2,1,0:T(8,128)(2,1)S(1)}, bf16[8,128,128]{2,1,0:T(8,128)(2,1)S(1)}, u32[]{:S(2)}, u32[]{:S(2)}) collective-permute-start(bf16[8,128,128]{2,1,0:T(8,128)(2,1)S(1)} %all_to_all.51.own_ref), channel_id=1, source_target_pairs={{0,4},{4,0},{1,5},{5,1},{2,6},{6,2},{3,7},{7,3},{8,12},{12,8},{9,1... | collective-permute-start | bytes 786440 | tf_op jit(solution)/shard_map/ppermute | solution.py:351
  179.9 8.5 %shard_map.52 = bf16[128,128,128]{2,1,0:T(8,128)(2,1)} custom-call(bf16[128,128,128]{2,1,0:T(8,128)(2,1)} %get-tuple-element.30.u_hbm, bf16[8,128,128]{2,1,0:T(8,128)(2,1)S(1)} %all_to_all.51.own_ref, bf16[8,128,128]{2,1,0:T(8,128)(2,1)S(1)} %collective-permute-done.5.oth_ref, bf16[256,64]{1,0:T(8,128)(2,1)S(1)} %get-tuple-element.23.ix_ref, ...), custom_call_target="tpu_custom_call" | custom-call | tf_op jit(solution)/shard_map/pallas_call | solution.py:283
  (32 shorter events, 7.1 us)
Async XLA Ops:
  6.5 104.4 %all-gather.5.cloned.1.call-start = ((), (), s32[]{:S(2)}) async-start(), calls=%async_computation.9 | async-start | bytes 4456448 | tf_op jit(solution)/shard_map/all_gather | solution.py:309
  8.6 140.6 %all-gather.7.cloned.1.call-start = ((), (), s32[]{:S(2)}) async-start(), calls=%async_computation.10 | async-start | bytes 4456448 | tf_op jit(solution)/shard_map/all_gather | solution.py:309
  9.7 76.1 %copy-start.1 = (f32[3,128]{1,0:T(4,128)S(1)}, f32[3,128]{1,0:T(4,128)}, u32[]{:S(2)}) copy-start(f32[3,128]{1,0:T(4,128)} %param.7) | copy-start | bytes 4612
  9.8 76.1 %copy-start = (bf16[3,128,128]{2,1,0:T(8,128)(2,1)S(1)}, bf16[3,128,128]{2,1,0:T(8,128)(2,1)}, u32[]{:S(2)}) copy-start(bf16[3,128,128]{2,1,0:T(8,128)(2,1)} %param.6) | copy-start | bytes 294916
  14.3 8.3 %collective-permute-start = (bf16[8,128,128]{2,1,0:T(8,128)(2,1)S(1)}, bf16[8,128,128]{2,1,0:T(8,128)(2,1)S(1)}, u32[]{:S(2)}, u32[]{:S(2)}) collective-permute-start(bf16[8,128,128]{2,1,0:T(8,128)(2,1)S(1)} %get-tuple-element.20), channel_id=1, source_target_pairs={{0,4},{4,0},{1,5},{5,1},{2,6},{6,2},{3,7},{7,3},{8,12},{12,8},{9,1... | collective-permute-start | bytes 786440 | tf_op jit(solution)/shard_map/ppermute | solution.py:330
  15.8 15.2 %all-to-all-start = ((bf16[16,2,2,2,8,128]{5,4,3,2,1,0:T(8,128)(2,1)}), bf16[16,2,2,2,8,128]{5,4,3,2,1,0:T(8,128)(2,1)S(1)}, u32[]{:S(2)}, u32[]{:S(2)}) async-start(bf16[16,2,2,2,8,128]{5,4,3,2,1,0:T(8,128)(2,1)} %bitcast.15), calls=%async_computation | async-start | bytes 524288 | tf_op jit(solution)/shard_map/all_to_all | solution.py:313
  78.5 8.5 %collective-permute-start.1 = (bf16[8,128,128]{2,1,0:T(8,128)(2,1)S(1)}, bf16[8,128,128]{2,1,0:T(8,128)(2,1)S(1)}, u32[]{:S(2)}, u32[]{:S(2)}) collective-permute-start(bf16[8,128,128]{2,1,0:T(8,128)(2,1)S(1)} %all_to_all.48.own_ref), channel_id=1, source_target_pairs={{0,4},{4,0},{1,5},{5,1},{2,6},{6,2},{3,7},{7,3},{8,12},{12,8},{9,1... | collective-permute-start | bytes 786440 | tf_op jit(solution)/shard_map/ppermute | solution.py:351
  96.5 1.6 collective-permute-start.2
  128.6 4.0 %collective-permute-start.3 = (bf16[8,128,128]{2,1,0:T(8,128)(2,1)S(1)}, bf16[8,128,128]{2,1,0:T(8,128)(2,1)S(1)}, u32[]{:S(2)}, u32[]{:S(2)}) collective-permute-start(bf16[8,128,128]{2,1,0:T(8,128)(2,1)S(1)} %all_to_all.50.own_ref), channel_id=1, source_target_pairs={{0,4},{4,0},{1,5},{5,1},{2,6},{6,2},{3,7},{7,3},{8,12},{12,8},{9,1... | collective-permute-start | bytes 786440 | tf_op jit(solution)/shard_map/ppermute | solution.py:351
  142.2 1.7 collective-permute-start.4
  144.6 13.6 %all-to-all-start.7 = ((bf16[8,128,128]{2,1,0:T(8,128)(2,1)}), bf16[8,128,128]{2,1,0:T(8,128)(2,1)S(1)}, u32[]{:S(2)}, u32[]{:S(2)}) async-start(bf16[8,128,128]{2,1,0:T(8,128)(2,1)} %add_convert_fusion), calls=%async_computation.7 | async-start | bytes 524288 | tf_op jit(solution)/shard_map/all_to_all | solution.py:334
  175.8 4.1 %collective-permute-start.5 = (bf16[8,128,128]{2,1,0:T(8,128)(2,1)S(1)}, bf16[8,128,128]{2,1,0:T(8,128)(2,1)S(1)}, u32[]{:S(2)}, u32[]{:S(2)}) collective-permute-start(bf16[8,128,128]{2,1,0:T(8,128)(2,1)S(1)} %all_to_all.51.own_ref), channel_id=1, source_target_pairs={{0,4},{4,0},{1,5},{5,1},{2,6},{6,2},{3,7},{7,3},{8,12},{12,8},{9,1... | collective-permute-start | bytes 786440 | tf_op jit(solution)/shard_map/ppermute | solution.py:351
Sparse Core Ops, SparseCore 0:
  9.7 65.6 all-gather.4
  77.8 60.6 all-gather.6

commit v2 on v1

--- a/solution.py
+++ b/solution.py
@@ -18,6 +18,15 @@
 RC = 4 * KY
 SC = RC + 4
 SG = 2 * KY + 4
+
+SIDE = 4
+SLICE = 32
+
+
+def shift(dy, dx):
+    return [
+        (y * SIDE + x, (y + dy) % SIDE * SIDE + (x + dx) % SIDE) for y in range(SIDE) for x in range(SIDE)
+    ]
 
 
 def grid_index(z, core):
@@ -48,15 +57,12 @@
     return jnp.dot(a, b, preferred_element_type=jnp.float32)
 
 
-GROUP = 8
-BLOCK = 16
-
-
-def copies_in(hbm, buf, sems):
-    return [
-        pltpu.make_async_copy(hbm.at[pl.ds(n * BLOCK, BLOCK)], buf.at[pl.ds(n * BLOCK, BLOCK)], sems.at[n])
-        for n in range(buf.shape[0] // BLOCK)
-    ]
+GROUP = 16
+
+
+def copy_in(hbm, buf, sems, i):
+    rows = pl.ds(i * GROUP, GROUP)
+    return pltpu.make_async_copy(hbm.at[rows], buf.at[rows], sems.at[i])
 
 
 def forward_group(i, u_ref, fy, h_ref):
@@ -99,9 +105,9 @@
     keep_ref, send_ref, fx_ref, ix_ref, fy_ref, iy_ref,
     u_buf, h_ref, m_ref, sems,
 ):
-    loads = copies_in(u_hbm, u_buf, sems)
-    for c in loads:
-        c.start()
+    steps = u_buf.shape[0] // GROUP
+    for i in range(steps):
+        copy_in(u_hbm, u_buf, sems, i).start()
     cx, cy = cos_ref[:KX], cos_ref[KX:]
     sx, sy = sin_ref[:KX], sin_ref[KX:]
     bf16 = jnp.bfloat16
@@ -115,26 +121,27 @@
     fy_ref[...] = jnp.concatenate([cy, -sy], axis=0).astype(bf16)
     double = jnp.where(lax.broadcasted_iota(jnp.int32, (KY, 128), 0) == 0, 1.0, 2.0)
     iy_ref[...] = jnp.concatenate([double * cy, -(double * sy), blank], axis=0).T.astype(bf16)
-    per = BLOCK // GROUP
-
-    for n, c in enumerate(loads):
-        c.wait()
-
-        def step(i, carry):
-            forward_group(i, u_buf, fy_ref[...], h_ref)
-            return carry
-
-        lax.fori_loop(n * per, (n + 1) * per, step, 0)
+
+    def step(i, carry):
+        copy_in(u_hbm, u_buf, sems, i).wait()
+        forward_group(i, u_buf, fy_ref[...], h_ref)
+        return carry
+
+    lax.fori_loop(0, steps, step, 0)
     modes_of(h_ref, m_ref, fx_ref, keep_ref, send_ref)
 
 
 def layer_body(u_hbm, own_ref, oth_ref, ix_ref, iy_ref, w_ref, b_ref, out_hbm, u_buf, bs_ref, g_ref, sems, forward):
-    loads = copies_in(u_hbm, u_buf, sems.at[0])
-    for c in loads:
-        c.start()
-    for k in range(ZN):
+    steps = u_buf.shape[0] // GROUP
+    for i in range(steps):
+        copy_in(u_hbm, u_buf, sems.at[0], i).start()
+
+    def unpack(k, carry):
         bs_ref[pl.ds(k * SC, RC), :] = own_ref[k].astype(jnp.float32)
         bs_ref[pl.ds((ZN + k) * SC, RC), :] = oth_ref[k].astype(jnp.float32)
+        return carry
+
+    lax.fori_loop(0, ZN, unpack, 0)
     scale = 1.0 / math.sqrt(2 * KX * KY)
     ix = ix_ref[...]
     for q in range(0, KY, 2):
@@ -151,9 +158,6 @@
             g = dot(ix[128 * part : 128 * part + 128], rhs) * scale
             for d in range(2):
                 g_ref[pl.ds(part * KY + q + d, 128, stride=SG), :] = g[:, 128 * d : 128 * d + 128]
-    for c in loads:
-        c.wait()
-    steps = u_buf.shape[0] // GROUP
 
     def store(i):
         return pltpu.make_async_copy(
@@ -175,12 +179,14 @@
             u_buf[x] = (half + half * lax.erf(z * math.sqrt(0.5))).astype(jnp.bfloat16)
 
     def step(i, carry):
+        copy_in(u_hbm, u_buf, sems.at[0], i).wait()
         if forward is not None:
             forward(i - 1)
         point(i)
         store(i).start()
         return carry
 
+    copy_in(u_hbm, u_buf, sems.at[0], 0).wait()
     point(0)
     store(0).start()
     lax.fori_loop(1, steps, step, 0)
@@ -216,48 +222,98 @@
     )()
 
 
-def few_kernel(a_ref, w_ref, out_ref, as_ref, bs_ref):
-    members = a_ref.shape[0]
-    as_ref[...] = a_ref[...].astype(jnp.float32).reshape(members * 8, 128)
-    for e in range(2):
+def split_kernel(spectral_hbm, first_ref, *refs):
+    outs, buf, sems = refs[:-2], refs[-2], refs[-1]
+    first = pltpu.make_async_copy(spectral_hbm.at[0], first_ref, sems.at[0, 0])
+    loads = [pltpu.make_async_copy(spectral_hbm.at[n + 1], buf.at[n], sems.at[0, n + 1]) for n in range(len(outs))]
+    stores = [pltpu.make_async_copy(buf.at[n], out, sems.at[1, n + 1]) for n, out in enumerate(outs)]
+    for c in loads:
+        c.start()
+    first.start()
+    for load, store in zip(loads, stores):
+        load.wait()
+        store.start()
+    first.wait()
+    for c in stores:
+        c.wait()
+
+
+def turn_kernel(s_ref, *refs):
+    outs, t_ref = refs[:-1], refs[-1]
+    a = s_ref[0].astype(jnp.float32)
+    for k in range(1, ZN):
+        a = a + s_ref[k].astype(jnp.float32)
+    t_ref[...] = a.T
+    y = lax.axis_index("mem") // SIDE
+    for k in range(SIDE):
+        start = pl.multiple_of((y + k) % SIDE * SLICE, SLICE)
+        outs[k][...] = t_ref[pl.ds(start, SLICE), :].astype(jnp.bfloat16)
+
+
+def share_kernel(*refs):
+    a_refs, w_refs, outs = refs[:SIDE], refs[SIDE : 2 * SIDE], refs[2 * SIDE : 3 * SIDE]
+    t_ref, m_ref, w_buf, sems = refs[3 * SIDE :]
+    x = lax.axis_index("mem") % SIDE
+    loads = [
+        pltpu.make_async_copy(w_refs[k], w_buf.at[(x + SIDE - k) % SIDE], sems.at[k]) for k in range(SIDE)
+    ]
+    for c in loads:
+        c.start()
+    t_ref[...] = jnp.concatenate([r[...].astype(jnp.float32) for r in a_refs], axis=0).T
+    row = lax.broadcasted_iota(jnp.int32, (8, 128), 0)
+    lane = lax.broadcasted_iota(jnp.int32, (8, 128), 1)
+    own = lane // SLICE == row
+    for c in loads:
+        c.wait()
+    for q in range(KY):
         for jj in range(2):
+            at = [q * 4 + 2 * ri + jj for ri in range(2)]
+            lhs = jnp.concatenate(
+                [jnp.where(own, t_ref[r : r + 1, :], 0.0) for r in at], axis=0
+            ).astype(jnp.bfloat16)
             w = jnp.concatenate(
                 [
-                    w_ref[:, jj, ri, e].astype(jnp.float32).reshape(128, 128).astype(jnp.bfloat16)
+                    jnp.concatenate([w_buf[x, jj, ri, q].astype(jnp.float32) for x in range(SIDE)] * SIDE, axis=0)
                     for ri in range(2)
                 ],
                 axis=1,
-            )
-            row_re = e * 4 + jj
-            row_im = e * 4 + 2 + jj
-            re = dot(as_ref[pl.ds(row_re, members, stride=8), :].astype(jnp.bfloat16), w)
-            im = dot(as_ref[pl.ds(row_im, members, stride=8), :].astype(jnp.bfloat16), w)
-            bs_ref[pl.ds(row_re, members, stride=8), :] = re[:, :128] - im[:, 128:]
-            bs_ref[pl.ds(row_im, members, stride=8), :] = re[:, 128:] + im[:, :128]
-    out_ref[...] = bs_ref[...].reshape(members, 8, 128).astype(jnp.bfloat16)
-
-
-def many_kernel(s_ref, w_hbm, out_ref, w_buf, sems):
+            ).astype(jnp.bfloat16)
+            out = dot(lhs, w)
+            re, im = out[:8], out[8:]
+            m_ref[pl.ds(at[0], 8, stride=SC), :] = re[:, :128] - im[:, 128:]
+            m_ref[pl.ds(at[1], 8, stride=SC), :] = re[:, 128:] + im[:, :128]
+    for k in range(SIDE):
+        outs[k][...] = m_ref[pl.ds(k * SC, RC), :].astype(jnp.bfloat16)
+
+
+def total_kernel(*refs):
+    out_ref = refs[-1]
+    b = refs[0][...].astype(jnp.float32)
+    for r in refs[1:-1]:
+        b = b + r[...].astype(jnp.float32)
+    b = b.astype(jnp.bfloat16)
+    for k in range(ZN):
+        out_ref[k] = b
+
+
+def many_kernel(a_ref, w_hbm, out_ref, w_buf, sems):
     loads = [
         pltpu.make_async_copy(w_hbm.at[:, :, pl.ds(4 * b, 4)], w_buf.at[b], sems.at[b])
         for b in range(KY // 4)
     ]
     for c in loads:
         c.start()
-    a = s_ref[0].astype(jnp.float32)
-    for k in range(1, ZN):
-        a = a + s_ref[k].astype(jnp.float32)
     row = lax.broadcasted_iota(jnp.int32, (16, 128), 0)
     lower = row % 4 < 2
     blocks = []
     for b in range(KY // 4):
-        rows = a[16 * b : 16 * b + 16]
+        rows = a_ref[16 * b : 16 * b + 16]
         acc = None
         loads[b].wait()
         for dq in range(4):
             for jj in range(2):
                 mine = (row == dq * 4 + jj) | (row == dq * 4 + 2 + jj)
-                lhs = jnp.where(mine, rows, 0.0).astype(jnp.bfloat16)
+                lhs = jnp.where(mine, rows, 0)
                 w = jnp.concatenate([w_buf[b, jj, 0, dq], w_buf[b, jj, 1, dq]], axis=1)
                 part = dot(lhs, w)
                 acc = part if acc is None else acc + part
@@ -273,9 +329,10 @@
 
 V = pl.BlockSpec(memory_space=pltpu.VMEM)
 H = pl.BlockSpec(memory_space=pltpu.HBM)
-
-
-def call(kernel, args, outs, scratch=(), in_hbm=(), out_hbm=(), alias=None, limit=24):
+A = pl.BlockSpec(memory_space=pl.ANY)
+
+
+def call(kernel, args, outs, scratch=(), in_hbm=(), out_hbm=(), anywhere=(), limit=24):
     args = [
         pltpu.with_memory_space_constraint(a, pltpu.HBM) if i in in_hbm else a for i, a in enumerate(args)
     ]
@@ -283,10 +340,9 @@
     return pl.pallas_call(
         kernel,
         out_shape=outs,
-        in_specs=[H if i in in_hbm else V for i in range(len(args))],
+        in_specs=[H if i in in_hbm else A if i in anywhere else V for i in range(len(args))],
         out_specs=[H if i in out_hbm else V for i in range(len(outs))],
         scratch_shapes=list(scratch),
-        input_output_aliases=alias or {},
         compiler_params=pltpu.CompilerParams(vmem_limit_bytes=limit << 20),
     )(*args)
 
@@ -294,7 +350,6 @@
 def local(field, spectral, pointwise, bias):
     u = field[0]
     rows_here, cols_here, channels = u.shape
-    members = lax.axis_size("mem")
     bf16, f32 = jnp.bfloat16, jnp.float32
     sds = jax.ShapeDtypeStruct
     dma = pltpu.SemaphoreType.DMA
@@ -303,14 +358,20 @@
     bs = pltpu.VMEM((2 * ZN * SC, channels), f32)
     gs = pltpu.VMEM((rows_here * SG, channels), f32)
     hs = pltpu.VMEM((2 * KY * SC, channels), f32)
-    blocks, steps = rows_here // BLOCK, rows_here // GROUP
-
-    weights = {
-        level: lax.all_gather(spectral[level], "mem", axis=3, tiled=True) for level in range(1, LAYERS)
-    }
-    first = spectral[0].reshape(2, 2, members, 2, 8, channels)
-    first = jnp.moveaxis(first, 2, 0)
-    first = lax.all_to_all(first, "mem", 0, 0, tiled=True)
+    steps = rows_here // GROUP
+
+    level_weights = sds(spectral.shape[1:], bf16)
+    split = call(
+        split_kernel, (spectral,), [level_weights] * LAYERS,
+        (pltpu.VMEM((LAYERS - 1, *spectral.shape[1:]), bf16), dma((2, LAYERS))),
+        in_hbm=(0,), out_hbm=tuple(range(1, LAYERS)),
+    )
+    weights = {}
+    for level in range(1, LAYERS):
+        weights[level] = lax.all_gather(split[level], "mem", axis=3, tiled=True)
+    near = [split[0]]
+    for k in range(1, SIDE):
+        near.append(lax.ppermute(split[0], "mem", shift(0, k)))
 
     cosines, sines = angle_tables(rows_here, cols_here)
     keep, send, forward_x, inverse_x, forward_y, inverse_y = call(
@@ -323,26 +384,36 @@
             sds((2 * KY, cols_here), bf16),
             sds((cols_here, 128), bf16),
         ],
-        (ub, hs, bs, dma((blocks,))),
+        (ub, hs, bs, dma((steps,))),
         in_hbm=(0,),
     )
     for level in range(LAYERS):
         other = lax.ppermute(send, GRID, PAIR)
         paired = (keep + other.astype(f32)).astype(bf16)
-        if level == 0:
-            paired, first = lax.optimization_barrier((paired, first))
         parts = lax.all_to_all(paired, GRID, 0, 0, axis_index_groups=LINES, tiled=True)
         if level == 0:
-            coeffs = parts.astype(f32).sum(axis=0).astype(bf16).reshape(members, 8, channels)
-            coeffs = lax.all_to_all(coeffs, "mem", 0, 0, tiled=True)
-            small = pltpu.VMEM((members * 8, channels), f32)
-            (mixed,) = call(few_kernel, (coeffs, first), [sds((members, 8, channels), bf16)], (small, small))
-            mixed = lax.all_to_all(mixed, "mem", 0, 0, tiled=True).reshape(RC, channels)
-            mixed = jnp.broadcast_to(mixed, (ZN, RC, channels))
+            square = pltpu.VMEM((RC, channels), f32)
+            slices = call(turn_kernel, (parts,), [sds((SLICE, RC), bf16)] * SIDE, (square,))
+            slices = [slices[0]] + [lax.ppermute(slices[k], "mem", shift(k, 0)) for k in range(1, SIDE)]
+            shares = call(
+                share_kernel,
+                (*slices, *near),
+                [sds((RC, channels), bf16)] * SIDE,
+                (
+                    square,
+                    pltpu.VMEM((8 * SC, channels), f32),
+                    pltpu.VMEM((SIDE, *spectral.shape[1:]), bf16),
+                    dma((SIDE,)),
+                ),
+                anywhere=tuple(range(SIDE, 2 * SIDE)),
+            )
+            shares = [shares[0]] + [lax.ppermute(shares[k], "mem", shift(-k, 0)) for k in range(1, SIDE)]
+            (mixed,) = call(total_kernel, shares, [sds((ZN, RC, channels), bf16)])
         else:
+            coeffs = parts.astype(f32).sum(axis=0).astype(bf16)
             (mixed,) = call(
                 many_kernel,
-                (parts, weights[level]),
+                (coeffs, weights[level]),
                 [sds((ZN, RC, channels), bf16)],
                 (pltpu.VMEM((KY // 4, 2, 2, 4, channels, channels), bf16), dma((KY // 4,))),
                 in_hbm=(1,),

time: 198 us -> 180 us (0.909)
  blocking collectives: 88.9 us -> 69 us
  starting transfers between devices: 26.2 us -> 34.4 us
  Pallas kernels: 38.6 us -> 30.5 us
  waiting for transfers between devices: 23.9 us -> 28.4 us
  local copies, waits for them, and re-layouts: 2.81 us -> 0.03 us
    all_to_all x2 -> x0, blocking collectives: 18.7 us -> none  [the longest x1 9.5 us: local(): mixed = lax.all_to_all(mixed, 'mem', 0, 0, tiled=True).reshape(RC, channels)]
    ppermute x0 -> x9, starting transfers between devices: none -> 13.9 us  [the longest x3 5.08 us: local(): lax.ppermute(slices[k], 'mem', shift(k, 0))]
    ppermute x0 -> x9, waiting for transfers between devices: none -> 9.38 us  [the longest x3 5.77 us: local(): near.append(lax.ppermute(split[0], 'mem', shift(0, k)))]
    all_to_all x1 -> x0, waiting for transfers between devices: 8.41 us -> none  [local(): first = lax.all_to_all(first, 'mem', 0, 0, tiled=True)]
    pallas_call x7 -> x10, Pallas kernels: 38.6 us -> 30.5 us  [call(): pl.pallas_call(kernel, out_shape=outs, in_specs=[H if i in in_hbm else A...]
    all_gather x2, waiting for transfers between devices: 0.01 us -> 7.73 us  [local(): weights[level] = lax.all_gather(split[level], 'mem', axis=3, tiled=True)]
    all_to_all x1 -> x0, starting transfers between devices: 6.75 us -> none  [local(): first = lax.all_to_all(first, 'mem', 0, 0, tiled=True)]
    all_to_all x1, waiting for transfers between devices: 9.01 us -> 3.7 us  [local(): lax.all_to_all(paired, GRID, 0, 0, axis_index_groups=LINES, tiled=True)]
  transfers between devices with their start and end apart: 10 -> 18, of which waited for: 7 -> 11; matrix products, arithmetic and copies ran while one was open for 1% -> 1% of each run, Pallas kernels for 14% -> 11%
where the time goes in v2:
time: 180 us; the launch traced here: 177 us
  blocking collectives  69 us (38%)
  starting transfers between devices  34.4 us (19%)
  Pallas kernels  30.5 us (17%)
  waiting for transfers between devices  28.4 us (16%)
  between operations  13.6 us (8%)
    all_to_all x3, blocking collectives, local(): own = lax.all_to_all(mixed, GRID, 0, 0, axis_index_groups=LINES, tiled=True)  43.8 us
    pallas_call x10, Pallas kernels, call(): pl.pallas_call(kernel, out_shape=outs, in_specs=[H if i in in_hbm else A...  30.5 us
    all_to_all x2, blocking collectives, local(): lax.all_to_all(paired, GRID, 0, 0, axis_index_groups=LINES, tiled=True)  25.3 us
    ppermute x3, starting transfers between devices, local(): oth = lax.ppermute(own, GRID, PAIR)  10.6 us
    all_to_all x1, starting transfers between devices, local(): lax.all_to_all(paired, GRID, 0, 0, axis_index_groups=LINES, tiled=True)  8.01 us
    all_gather x2, waiting for transfers between devices, local(): weights[level] = lax.all_gather(split[level], 'mem', axis=3, tiled=True)  7.73 us
    ppermute x3, waiting for transfers between devices, local(): near.append(lax.ppermute(split[0], 'mem', shift(0, k)))  5.77 us
    ppermute x3, starting transfers between devices, local(): lax.ppermute(slices[k], 'mem', shift(k, 0))  5.08 us
  transfers between devices with their start and end apart: 18, of which 11 were waited for; matrix products, arithmetic and copies ran while one was open for 1% of the time, Pallas kernels for 11%

profile of v2, /device:TPU:33, one launch (start us, length us, event | category | flops | bytes accessed | tf_op | source)
XLA Modules:
  0.0 177.2 jit_solution(18113394615237974468)
XLA Ops:
  6.5 1.9 %shard_map.48 = (bf16[2,2,32,8,128]{4,3,2,1,0:T(8,128)(2,1)S(1)}, bf16[2,2,32,8,128]{4,3,2,1,0:T(8,128)(2,1)}, bf16[2,2,32,8,128]{4,3,2,1,0:T(8,128)(2,1)}) custom-call(bf16[3,2,2,32,8,128]{5,4,3,2,1,0:T(8,128)(2,1)} %spectral_hbm.1), custom_call_target="tpu_custom_call" | custom-call | tf_op jit(solution)/shard_map/pallas_call | solution.py:340
  9.6 3.4 %shard_map.46 = (f32[8,128,128]{2,1,0:T(8,128)S(1)}, bf16[8,128,128]{2,1,0:T(8,128)(2,1)S(1)}, bf16[64,256]{1,0:T(8,128)(2,1)S(1)}, bf16[256,64]{1,0:T(8,128)(2,...) custom-call(bf16[128,128,128]{2,1,0:T(8,128)(2,1)} %bitcast.8, ...), custom_call_target="tpu_custom_call" | custom-call | tf_op jit(solution)/shard_map/pallas_call | solution.py:340
  15.7 8.0 %all-to-all-start = ((bf16[8,128,128]{2,1,0:T(8,128)(2,1)}), bf16[8,128,128]{2,1,0:T(8,128)(2,1)S(1)}, u32[]{:S(2)}, u32[]{:S(2)}) async-start(bf16[8,128,128]{2,1,0:T(8,128)(2,1)} %add_convert_fusion.2), calls=%async_computation | async-start | bytes 524288 | tf_op jit(solution)/shard_map/all_to_all | solution.py:393
  24.9 2.4 %collective-permute-start.5 = (bf16[2,2,32,8,128]{4,3,2,1,0:T(8,128)(2,1)S(1)}, bf16[2,2,32,8,128]{4,3,2,1,0:T(8,128)(2,1)S(1)}, u32[]{:S(2)}, u32[]{:S(2)}) collective-permute-start(bf16[2,2,32,8,128]{4,3,2,1,0:T(8,128)(2,1)S(1)} %get-tuple-element.34.refs_4_), channel_id=1, source_target_pairs={{0,32},{16,48},{32,0},{48,16},{64,96},{80,112},{96,64},{112,80},{1... | collective-permute-start | bytes 786440 | tf_op jit(solution)/shard_map/ppermute | solution.py:374
  28.5 3.7 %all-to-all-done.s_ref = bf16[8,128,128]{2,1,0:T(8,128)(2,1)S(1)} async-done(((bf16[8,128,128]{2,1,0:T(8,128)(2,1)}), bf16[8,128,128]{2,1,0:T(8,128)(2,1)S(1)}, u32[]{:S(2)}, u32[]{:S(2)}) %all-to-all-start) | async-done | bytes 262176 | tf_op jit(solution)/shard_map/all_to_all | solution.py:393
  32.3 1.4 collective-permute-start.1
  33.7 2.6 %collective-permute-start.2 = (bf16[32,128]{1,0:T(8,128)(2,1)S(1)}, bf16[32,128]{1,0:T(8,128)(2,1)S(1)}, u32[]{:S(2)}, u32[]{:S(2)}) collective-permute-start(bf16[32,128]{1,0:T(8,128)(2,1)S(1)} %get-tuple-element.32), channel_id=1, source_target_pairs={{0,128},{16,144},{32,160},{48,176},{64,192},{80,208},{96,224},{112... | collective-permute-start | bytes 24584 | tf_op jit(solution)/shard_map/ppermute | solution.py:397
  37.4 5.8 %collective-permute-done.5.refs_6_ = bf16[2,2,32,8,128]{4,3,2,1,0:T(8,128)(2,1)S(1)} collective-permute-done((bf16[2,2,32,8,128]{4,3,2,1,0:T(8,128)(2,1)S(1)}, bf16[2,2,32,8,128]{4,3,2,1,0:T(8,128)(2,1)S(1)}, u32[]{:S(2)}, u32[]{:S(2)}) %collective-permute-start.5) | collective-permute-done | bytes 262176 | tf_op jit(solution)/shard_map/ppermute | solution.py:374
  44.2 3.0 %collective-permute-start.7 = (bf16[128,128]{1,0:T(8,128)(2,1)S(1)}, bf16[128,128]{1,0:T(8,128)(2,1)S(1)}, u32[]{:S(2)}, u32[]{:S(2)}) collective-permute-start(bf16[128,128]{1,0:T(8,128)(2,1)S(1)} %get-tuple-element.36), channel_id=1, source_target_pairs={{0,192},{16,208},{32,224},{48,240},{64,0},{80,16},{96,32},{112,48}... | collective-permute-start | bytes 98312 | tf_op jit(solution)/shard_map/ppermute | solution.py:410
  48.2 3.3 %collective-permute-done.8.refs_2_ = bf16[128,128]{1,0:T(8,128)(2,1)S(1)} collective-permute-done((bf16[128,128]{1,0:T(8,128)(2,1)S(1)}, bf16[128,128]{1,0:T(8,128)(2,1)S(1)}, u32[]{:S(2)}, u32[]{:S(2)}) %collective-permute-start.8) | collective-permute-done | bytes 32800 | tf_op jit(solution)/shard_map/ppermute | solution.py:410
  51.8 14.4 %all_to_all.30.own_ref = bf16[8,128,128]{2,1,0:T(8,128)(2,1)S(1)} all-to-all(bf16[8,128,128]{2,1,0:T(8,128)(2,1)S(1)} %shard_map.50), channel_id=1, replica_groups={{0,1,2,3,8,9,10,11},{4,5,6,7,12,13,14,15},{16,17,18,19,24,25,26,27},{20..., dimensions={0} | all-to-all | bytes 524288 | tf_op jit(solution)/shard_map/all_to_all | solution.py:421
  66.2 4.2 %collective-permute-start.10 = (bf16[8,128,128]{2,1,0:T(8,128)(2,1)S(1)}, bf16[8,128,128]{2,1,0:T(8,128)(2,1)S(1)}, u32[]{:S(2)}, u32[]{:S(2)}) collective-permute-start(bf16[8,128,128]{2,1,0:T(8,128)(2,1)S(1)} %all_to_all.30.own_ref), channel_id=1, source_target_pairs={{0,4},{4,0},{1,5},{5,1},{2,6},{6,2},{3,7},{7,3},{8,12},{12,8},{9,1... | collective-permute-start | bytes 786440 | tf_op jit(solution)/shard_map/ppermute | solution.py:422
  71.5 6.1 %shard_map.51 = (bf16[128,128,128]{2,1,0:T(8,128)(2,1)}, f32[8,128,128]{2,1,0:T(8,128)S(1)}, bf16[8,128,128]{2,1,0:T(8,128)(2,1)S(1)}) custom-call(bf16[128,128,128]{2,1,0:T(8,128)(2,1)} %bitcast.9, bf16[8,128,128]{2,1,0:T(8,128)(2,1)S(1)} %all_to_all.30.own_ref, bf16[8,128,128]{2,1,0:T(8,128)(2,1)S(1)} %collective-permute-done.10.oth_ref, ...), custom_call_target="tpu_custom_call" | custom-call | tf_op jit(solution)/shard_map/pallas_call | solution.py:340
  79.5 12.6 %all_to_all.31 = bf16[8,128,128]{2,1,0:T(8,128)(2,1)S(1)} all-to-all(bf16[8,128,128]{2,1,0:T(8,128)(2,1)S(1)} %add_convert_fusion.1), channel_id=1, replica_groups={{0,1,2,3,8,9,10,11},{4,5,6,7,12,13,14,15},{16,17,18,19,24,25,26,27},{20..., dimensions={0} | all-to-all | bytes 524288 | tf_op jit(solution)/shard_map/all_to_all | solution.py:393
  92.2 3.2 %shard_map.52 = bf16[8,128,128]{2,1,0:T(8,128)(2,1)S(1)} custom-call(bf16[128,128]{1,0:T(8,128)(2,1)S(1)} %reduce_sum.24.a_ref, bf16[2,2,32,128,128]{4,3,2,1,0:T(8,128)(2,1)} %all-gather.3.cloned.1.call-done.w_hbm), custom_call_target="tpu_custom_call" | custom-call | tf_op jit(solution)/shard_map/pallas_call | solution.py:340
  95.4 14.4 %all_to_all.32.own_ref = bf16[8,128,128]{2,1,0:T(8,128)(2,1)S(1)} all-to-all(bf16[8,128,128]{2,1,0:T(8,128)(2,1)S(1)} %shard_map.52), channel_id=1, replica_groups={{0,1,2,3,8,9,10,11},{4,5,6,7,12,13,14,15},{16,17,18,19,24,25,26,27},{20..., dimensions={0} | all-to-all | bytes 524288 | tf_op jit(solution)/shard_map/all_to_all | solution.py:421
  109.8 3.0 %collective-permute-start.12 = (bf16[8,128,128]{2,1,0:T(8,128)(2,1)S(1)}, bf16[8,128,128]{2,1,0:T(8,128)(2,1)S(1)}, u32[]{:S(2)}, u32[]{:S(2)}) collective-permute-start(bf16[8,128,128]{2,1,0:T(8,128)(2,1)S(1)} %all_to_all.32.own_ref), channel_id=1, source_target_pairs={{0,4},{4,0},{1,5},{5,1},{2,6},{6,2},{3,7},{7,3},{8,12},{12,8},{9,1... | collective-permute-start | bytes 786440 | tf_op jit(solution)/shard_map/ppermute | solution.py:422
  113.9 6.2 %shard_map.53 = (bf16[128,128,128]{2,1,0:T(8,128)(2,1)}, f32[8,128,128]{2,1,0:T(8,128)S(1)}, bf16[8,128,128]{2,1,0:T(8,128)(2,1)S(1)}) custom-call(bf16[128,128,128]{2,1,0:T(8,128)(2,1)} %get-tuple-element.43.u_hbm, bf16[8,128,128]{2,1,0:T(8,128)(2,1)S(1)} %all_to_all.32.own_ref, bf16[8,128,128]{2,1,0:T(8,128)(2,1)S(1)} %collective-permute-done.12.oth_ref, ...), custom_call_target="tpu_custom_call" | custom-call | tf_op jit(solution)/shard_map/pallas_call | solution.py:340
  121.8 12.6 %all_to_all.33 = bf16[8,128,128]{2,1,0:T(8,128)(2,1)S(1)} all-to-all(bf16[8,128,128]{2,1,0:T(8,128)(2,1)S(1)} %add_convert_fusion), channel_id=1, replica_groups={{0,1,2,3,8,9,10,11},{4,5,6,7,12,13,14,15},{16,17,18,19,24,25,26,27},{20..., dimensions={0} | all-to-all | bytes 524288 | tf_op jit(solution)/shard_map/all_to_all | solution.py:393
  134.5 7.7 %all-gather.5.cloned.1.call-done.w_hbm = bf16[2,2,32,128,128]{4,3,2,1,0:T(8,128)(2,1)} async-done(((bf16[2,2,32,8,128]{4,3,2,1,0:T(8,128)(2,1)}), bf16[2,2,32,128,128]{4,3,2,1,0:T(8,128)(2,1)}) %all-gather.5.cloned.1.call-update) | async-done | bytes 4194320 | tf_op jit(solution)/shard_map/all_gather | solution.py:371
  142.2 3.2 %shard_map.54 = bf16[8,128,128]{2,1,0:T(8,128)(2,1)S(1)} custom-call(bf16[128,128]{1,0:T(8,128)(2,1)S(1)} %reduce_sum.25.a_ref, bf16[2,2,32,128,128]{4,3,2,1,0:T(8,128)(2,1)} %all-gather.5.cloned.1.call-done.w_hbm), custom_call_target="tpu_custom_call" | custom-call | tf_op jit(solution)/shard_map/pallas_call | solution.py:340
  145.3 14.9 %all_to_all.34.own_ref = bf16[8,128,128]{2,1,0:T(8,128)(2,1)S(1)} all-to-all(bf16[8,128,128]{2,1,0:T(8,128)(2,1)S(1)} %shard_map.54), channel_id=1, replica_groups={{0,1,2,3,8,9,10,11},{4,5,6,7,12,13,14,15},{16,17,18,19,24,25,26,27},{20..., dimensions={0} | all-to-all | bytes 524288 | tf_op jit(solution)/shard_map/all_to_all | solution.py:421
  160.3 3.5 %collective-permute-start.14 = (bf16[8,128,128]{2,1,0:T(8,128)(2,1)S(1)}, bf16[8,128,128]{2,1,0:T(8,128)(2,1)S(1)}, u32[]{:S(2)}, u32[]{:S(2)}) collective-permute-start(bf16[8,128,128]{2,1,0:T(8,128)(2,1)S(1)} %all_to_all.34.own_ref), channel_id=1, source_target_pairs={{0,4},{4,0},{1,5},{5,1},{2,6},{6,2},{3,7},{7,3},{8,12},{12,8},{9,1... | collective-permute-start | bytes 786440 | tf_op jit(solution)/shard_map/ppermute | solution.py:422
  164.9 5.5 %shard_map.55 = bf16[128,128,128]{2,1,0:T(8,128)(2,1)} custom-call(bf16[128,128,128]{2,1,0:T(8,128)(2,1)} %get-tuple-element.47.u_hbm, bf16[8,128,128]{2,1,0:T(8,128)(2,1)S(1)} %all_to_all.34.own_ref, bf16[8,128,128]{2,1,0:T(8,128)(2,1)S(1)} %collective-permute-done.14.oth_ref, bf16[256,64]{1,0:T(8,128)(2,1)S(1)} %get-tuple-element.39.ix_ref, ...), custom_call_target="tpu_custom_call" | custom-call | tf_op jit(solution)/shard_map/pallas_call | solution.py:340
  (47 shorter events, 16.7 us)
Async XLA Ops:
  6.5 85.7 %all-gather.3.cloned.1.call-start = ((), (), s32[]{:S(2)}) async-start(), calls=%async_computation.6 | async-start | bytes 4456448 | tf_op jit(solution)/shard_map/all_gather | solution.py:371
  8.4 133.8 %all-gather.5.cloned.1.call-start = ((), (), s32[]{:S(2)}) async-start(), calls=%async_computation.7 | async-start | bytes 4456448 | tf_op jit(solution)/shard_map/all_gather | solution.py:371
  8.5 61.9 %copy-start.1 = (f32[3,128]{1,0:T(4,128)S(1)}, f32[3,128]{1,0:T(4,128)}, u32[]{:S(2)}) copy-start(f32[3,128]{1,0:T(4,128)} %param.7) | copy-start | bytes 4612
  8.5 61.9 %copy-start = (bf16[3,128,128]{2,1,0:T(8,128)(2,1)S(1)}, bf16[3,128,128]{2,1,0:T(8,128)(2,1)}, u32[]{:S(2)}) copy-start(bf16[3,128,128]{2,1,0:T(8,128)(2,1)} %param.6) | copy-start | bytes 294916
  13.0 1.9 %collective-permute-start = (bf16[8,128,128]{2,1,0:T(8,128)(2,1)S(1)}, bf16[8,128,128]{2,1,0:T(8,128)(2,1)S(1)}, u32[]{:S(2)}, u32[]{:S(2)}) collective-permute-start(bf16[8,128,128]{2,1,0:T(8,128)(2,1)S(1)} %get-tuple-element.29), channel_id=1, source_target_pairs={{0,4},{4,0},{1,5},{5,1},{2,6},{6,2},{3,7},{7,3},{8,12},{12,8},{9,1... | collective-permute-start | bytes 786440 | tf_op jit(solution)/shard_map/ppermute | solution.py:391
  15.7 16.5 %all-to-all-start = ((bf16[8,128,128]{2,1,0:T(8,128)(2,1)}), bf16[8,128,128]{2,1,0:T(8,128)(2,1)S(1)}, u32[]{:S(2)}, u32[]{:S(2)}) async-start(bf16[8,128,128]{2,1,0:T(8,128)(2,1)} %add_convert_fusion.2), calls=%async_computation | async-start | bytes 524288 | tf_op jit(solution)/shard_map/all_to_all | solution.py:393
  23.7 12.7 %collective-permute-start.4 = (bf16[2,2,32,8,128]{4,3,2,1,0:T(8,128)(2,1)S(1)}, bf16[2,2,32,8,128]{4,3,2,1,0:T(8,128)(2,1)S(1)}, u32[]{:S(2)}, u32[]{:S(2)}) collective-permute-start(bf16[2,2,32,8,128]{4,3,2,1,0:T(8,128)(2,1)S(1)} %get-tuple-element.34.refs_4_), channel_id=1, source_target_pairs={{0,16},{16,32},{32,48},{48,0},{64,80},{80,96},{96,112},{112,64},{1... | collective-permute-start | bytes 786440 | tf_op jit(solution)/shard_map/ppermute | solution.py:374
  24.9 18.3 %collective-permute-start.5 = (bf16[2,2,32,8,128]{4,3,2,1,0:T(8,128)(2,1)S(1)}, bf16[2,2,32,8,128]{4,3,2,1,0:T(8,128)(2,1)S(1)}, u32[]{:S(2)}, u32[]{:S(2)}) collective-permute-start(bf16[2,2,32,8,128]{4,3,2,1,0:T(8,128)(2,1)S(1)} %get-tuple-element.34.refs_4_), channel_id=1, source_target_pairs={{0,32},{16,48},{32,0},{48,16},{64,96},{80,112},{96,64},{112,80},{1... | collective-permute-start | bytes 786440 | tf_op jit(solution)/shard_map/ppermute | solution.py:374
  27.4 15.8 %collective-permute-start.6 = (bf16[2,2,32,8,128]{4,3,2,1,0:T(8,128)(2,1)S(1)}, bf16[2,2,32,8,128]{4,3,2,1,0:T(8,128)(2,1)S(1)}, u32[]{:S(2)}, u32[]{:S(2)}) collective-permute-start(bf16[2,2,32,8,128]{4,3,2,1,0:T(8,128)(2,1)S(1)} %get-tuple-element.34.refs_4_), channel_id=1, source_target_pairs={{0,48},{16,0},{32,16},{48,32},{64,112},{80,64},{96,80},{112,96},{1... | collective-permute-start | bytes 786440 | tf_op jit(solution)/shard_map/ppermute | solution.py:374
  32.3 10.9 %collective-permute-start.1 = (bf16[32,128]{1,0:T(8,128)(2,1)S(1)}, bf16[32,128]{1,0:T(8,128)(2,1)S(1)}, u32[]{:S(2)}, u32[]{:S(2)}) collective-permute-start(bf16[32,128]{1,0:T(8,128)(2,1)S(1)} %get-tuple-element.31), channel_id=1, source_target_pairs={{0,64},{16,80},{32,96},{48,112},{64,128},{80,144},{96,160},{112,17... | collective-permute-start | bytes 24584 | tf_op jit(solution)/shard_map/ppermute | solution.py:397
  33.7 9.5 %collective-permute-start.2 = (bf16[32,128]{1,0:T(8,128)(2,1)S(1)}, bf16[32,128]{1,0:T(8,128)(2,1)S(1)}, u32[]{:S(2)}, u32[]{:S(2)}) collective-permute-start(bf16[32,128]{1,0:T(8,128)(2,1)S(1)} %get-tuple-element.32), channel_id=1, source_target_pairs={{0,128},{16,144},{32,160},{48,176},{64,192},{80,208},{96,224},{112... | collective-permute-start | bytes 24584 | tf_op jit(solution)/shard_map/ppermute | solution.py:397
  36.4 6.9 %collective-permute-start.3 = (bf16[32,128]{1,0:T(8,128)(2,1)S(1)}, bf16[32,128]{1,0:T(8,128)(2,1)S(1)}, u32[]{:S(2)}, u32[]{:S(2)}) collective-permute-start(bf16[32,128]{1,0:T(8,128)(2,1)S(1)} %get-tuple-element.33), channel_id=1, source_target_pairs={{0,192},{16,208},{32,224},{48,240},{64,0},{80,16},{96,32},{112,48}... | collective-permute-start | bytes 24584 | tf_op jit(solution)/shard_map/ppermute | solution.py:397
  44.2 4.0 %collective-permute-start.7 = (bf16[128,128]{1,0:T(8,128)(2,1)S(1)}, bf16[128,128]{1,0:T(8,128)(2,1)S(1)}, u32[]{:S(2)}, u32[]{:S(2)}) collective-permute-start(bf16[128,128]{1,0:T(8,128)(2,1)S(1)} %get-tuple-element.36), channel_id=1, source_target_pairs={{0,192},{16,208},{32,224},{48,240},{64,0},{80,16},{96,32},{112,48}... | collective-permute-start | bytes 98312 | tf_op jit(solution)/shard_map/ppermute | solution.py:410
  47.1 4.4 %collective-permute-start.8 = (bf16[128,128]{1,0:T(8,128)(2,1)S(1)}, bf16[128,128]{1,0:T(8,128)(2,1)S(1)}, u32[]{:S(2)}, u32[]{:S(2)}) collective-permute-start(bf16[128,128]{1,0:T(8,128)(2,1)S(1)} %get-tuple-element.37), channel_id=1, source_target_pairs={{0,128},{16,144},{32,160},{48,176},{64,192},{80,208},{96,224},{112... | collective-permute-start | bytes 98312 | tf_op jit(solution)/shard_map/ppermute | solution.py:410
  47.4 4.3 %collective-permute-start.9 = (bf16[128,128]{1,0:T(8,128)(2,1)S(1)}, bf16[128,128]{1,0:T(8,128)(2,1)S(1)}, u32[]{:S(2)}, u32[]{:S(2)}) collective-permute-start(bf16[128,128]{1,0:T(8,128)(2,1)S(1)} %get-tuple-element.38), channel_id=1, source_target_pairs={{0,64},{16,80},{32,96},{48,112},{64,128},{80,144},{96,160},{112,17... | collective-permute-start | bytes 98312 | tf_op jit(solution)/shard_map/ppermute | solution.py:410
  66.2 5.3 %collective-permute-start.10 = (bf16[8,128,128]{2,1,0:T(8,128)(2,1)S(1)}, bf16[8,128,128]{2,1,0:T(8,128)(2,1)S(1)}, u32[]{:S(2)}, u32[]{:S(2)}) collective-permute-start(bf16[8,128,128]{2,1,0:T(8,128)(2,1)S(1)} %all_to_all.30.own_ref), channel_id=1, source_target_pairs={{0,4},{4,0},{1,5},{5,1},{2,6},{6,2},{3,7},{7,3},{8,12},{12,8},{9,1... | collective-permute-start | bytes 786440 | tf_op jit(solution)/shard_map/ppermute | solution.py:422
  77.7 1.8 %collective-permute-start.11 = (bf16[8,128,128]{2,1,0:T(8,128)(2,1)S(1)}, bf16[8,128,128]{2,1,0:T(8,128)(2,1)S(1)}, u32[]{:S(2)}, u32[]{:S(2)}) collective-permute-start(bf16[8,128,128]{2,1,0:T(8,128)(2,1)S(1)} %get-tuple-element.45), channel_id=1, source_target_pairs={{0,4},{4,0},{1,5},{5,1},{2,6},{6,2},{3,7},{7,3},{8,12},{12,8},{9,1... | collective-permute-start | bytes 786440 | tf_op jit(solution)/shard_map/ppermute | solution.py:391
  109.8 4.1 %collective-permute-start.12 = (bf16[8,128,128]{2,1,0:T(8,128)(2,1)S(1)}, bf16[8,128,128]{2,1,0:T(8,128)(2,1)S(1)}, u32[]{:S(2)}, u32[]{:S(2)}) collective-permute-start(bf16[8,128,128]{2,1,0:T(8,128)(2,1)S(1)} %all_to_all.32.own_ref), channel_id=1, source_target_pairs={{0,4},{4,0},{1,5},{5,1},{2,6},{6,2},{3,7},{7,3},{8,12},{12,8},{9,1... | collective-permute-start | bytes 786440 | tf_op jit(solution)/shard_map/ppermute | solution.py:422
  120.1 1.6 collective-permute-start.13
  160.3 4.6 %collective-permute-start.14 = (bf16[8,128,128]{2,1,0:T(8,128)(2,1)S(1)}, bf16[8,128,128]{2,1,0:T(8,128)(2,1)S(1)}, u32[]{:S(2)}, u32[]{:S(2)}) collective-permute-start(bf16[8,128,128]{2,1,0:T(8,128)(2,1)S(1)} %all_to_all.34.own_ref), channel_id=1, source_target_pairs={{0,4},{4,0},{1,5},{5,1},{2,6},{6,2},{3,7},{7,3},{8,12},{12,8},{9,1... | collective-permute-start | bytes 786440 | tf_op jit(solution)/shard_map/ppermute | solution.py:422
Sparse Core Ops, SparseCore 0:
  9.7 68.7 all-gather.2
  80.9 61.2 all-gather.4

commit v3 on v2

--- a/solution.py
+++ b/solution.py
@@ -57,7 +57,7 @@
     return jnp.dot(a, b, preferred_element_type=jnp.float32)
 
 
-GROUP = 16
+GROUP = 32
 
 
 def copy_in(hbm, buf, sems, i):
@@ -298,7 +298,7 @@
 
 def many_kernel(a_ref, w_hbm, out_ref, w_buf, sems):
     loads = [
-        pltpu.make_async_copy(w_hbm.at[:, :, pl.ds(4 * b, 4)], w_buf.at[b], sems.at[b])
+        pltpu.make_async_copy(w_hbm.at[:, :, :, pl.ds(4 * b, 4)], w_buf.at[b], sems.at[b])
         for b in range(KY // 4)
     ]
     for c in loads:
@@ -314,7 +314,13 @@
             for jj in range(2):
                 mine = (row == dq * 4 + jj) | (row == dq * 4 + 2 + jj)
                 lhs = jnp.where(mine, rows, 0)
-                w = jnp.concatenate([w_buf[b, jj, 0, dq], w_buf[b, jj, 1, dq]], axis=1)
+                w = jnp.concatenate(
+                    [
+                        w_buf[b, :, jj, ri, dq].astype(jnp.float32).reshape(128, 128).astype(jnp.bfloat16)
+                        for ri in range(2)
+                    ],
+                    axis=1,
+                )
                 part = dot(lhs, w)
                 acc = part if acc is None else acc + part
         straight = acc[:, :128]
@@ -367,8 +373,11 @@
         in_hbm=(0,), out_hbm=tuple(range(1, LAYERS)),
     )
     weights = {}
-    for level in range(1, LAYERS):
-        weights[level] = lax.all_gather(split[level], "mem", axis=3, tiled=True)
+
+    def gather(level, block):
+        weights[level] = lax.all_gather(block, "mem")
+
+    gather(1, split[1])
     near = [split[0]]
     for k in range(1, SIDE):
         near.append(lax.ppermute(split[0], "mem", shift(0, k)))
@@ -415,10 +424,16 @@
                 many_kernel,
                 (coeffs, weights[level]),
                 [sds((ZN, RC, channels), bf16)],
-                (pltpu.VMEM((KY // 4, 2, 2, 4, channels, channels), bf16), dma((KY // 4,))),
+                (
+                    pltpu.VMEM((KY // 4, lax.axis_size("mem"), 2, 2, 4, 8, channels), bf16),
+                    dma((KY // 4,)),
+                ),
                 in_hbm=(1,),
             )
         own = lax.all_to_all(mixed, GRID, 0, 0, axis_index_groups=LINES, tiled=True)
+        if level < LAYERS - 2:
+            own, block = lax.optimization_barrier((own, split[level + 2]))
+            gather(level + 2, block)
         oth = lax.ppermute(own, GRID, PAIR)
         args = (u, own, oth, inverse_x, inverse_y, pointwise[level], bias[level][None])
         if level < LAYERS - 1:

time: 180 us -> 170 us (0.944)
  waiting for transfers between devices: 28.4 us -> 20 us
    all_gather x2, waiting for transfers between devices: 7.73 us -> 0.43 us  [gather(): weights[level] = lax.all_gather(block, 'mem')]
where the time goes in v3:
time: 170 us; the launch traced here: 168 us
  blocking collectives  69.3 us (41%)
  starting transfers between devices  34.2 us (20%)
  Pallas kernels  29.1 us (17%)
  waiting for transfers between devices  20 us (12%)
  between operations  13.6 us (8%)
    all_to_all x3, blocking collectives, local(): own = lax.all_to_all(mixed, GRID, 0, 0, axis_index_groups=LINES, tiled=True)  44.2 us
    pallas_call x10, Pallas kernels, call(): pl.pallas_call(kernel, out_shape=outs, in_specs=[H if i in in_hbm else A...  29.1 us
    all_to_all x2, blocking collectives, local(): lax.all_to_all(paired, GRID, 0, 0, axis_index_groups=LINES, tiled=True)  25.2 us
    ppermute x3, starting transfers between devices, local(): oth = lax.ppermute(own, GRID, PAIR)  10.8 us
    all_to_all x1, starting transfers between devices, local(): lax.all_to_all(paired, GRID, 0, 0, axis_index_groups=LINES, tiled=True)  8.01 us
    ppermute x3, waiting for transfers between devices, local(): near.append(lax.ppermute(split[0], 'mem', shift(0, k)))  5.27 us
    ppermute x3, starting transfers between devices, local(): lax.ppermute(slices[k], 'mem', shift(k, 0))  5.05 us
    ppermute x3, starting transfers between devices, local(): near.append(lax.ppermute(split[0], 'mem', shift(0, k)))  4.81 us
  transfers between devices with their start and end apart: 18, of which 11 were waited for; matrix products, arithmetic and copies ran while one was open for 1% of the time, Pallas kernels for 11%

profile of v3, /device:TPU:33, one launch (start us, length us, event | category | flops | bytes accessed | tf_op | source)
XLA Modules:
  0.0 167.5 jit_solution(1520717510966047160)
XLA Ops:
  6.5 1.9 %shard_map.48 = (bf16[2,2,32,8,128]{4,3,2,1,0:T(8,128)(2,1)S(1)}, bf16[2,2,32,8,128]{4,3,2,1,0:T(8,128)(2,1)}, bf16[2,2,32,8,128]{4,3,2,1,0:T(8,128)(2,1)}) custom-call(bf16[3,2,2,32,8,128]{5,4,3,2,1,0:T(8,128)(2,1)} %spectral_hbm.1), custom_call_target="tpu_custom_call" | custom-call | tf_op jit(solution)/shard_map/pallas_call | solution.py:346
  8.8 3.1 %shard_map.46 = (f32[8,128,128]{2,1,0:T(8,128)S(1)}, bf16[8,128,128]{2,1,0:T(8,128)(2,1)S(1)}, bf16[64,256]{1,0:T(8,128)(2,1)S(1)}, bf16[256,64]{1,0:T(8,128)(2,...) custom-call(bf16[128,128,128]{2,1,0:T(8,128)(2,1)} %bitcast.10, ...), custom_call_target="tpu_custom_call" | custom-call | tf_op jit(solution)/shard_map/pallas_call | solution.py:346
  14.6 8.0 %all-to-all-start = ((bf16[8,128,128]{2,1,0:T(8,128)(2,1)}), bf16[8,128,128]{2,1,0:T(8,128)(2,1)S(1)}, u32[]{:S(2)}, u32[]{:S(2)}) async-start(bf16[8,128,128]{2,1,0:T(8,128)(2,1)} %add_convert_fusion.2), calls=%async_computation | async-start | bytes 524288 | tf_op jit(solution)/shard_map/all_to_all | solution.py:402
  22.6 1.2 collective-permute-start.4
  23.8 2.5 %collective-permute-start.5 = (bf16[2,2,32,8,128]{4,3,2,1,0:T(8,128)(2,1)S(1)}, bf16[2,2,32,8,128]{4,3,2,1,0:T(8,128)(2,1)S(1)}, u32[]{:S(2)}, u32[]{:S(2)}) collective-permute-start(bf16[2,2,32,8,128]{4,3,2,1,0:T(8,128)(2,1)S(1)} %get-tuple-element.36.refs_4_), channel_id=1, source_target_pairs={{0,32},{16,48},{32,0},{48,16},{64,96},{80,112},{96,64},{112,80},{1... | collective-permute-start | bytes 786440 | tf_op jit(solution)/shard_map/ppermute | solution.py:383
  27.4 3.7 %all-to-all-done.s_ref = bf16[8,128,128]{2,1,0:T(8,128)(2,1)S(1)} async-done(((bf16[8,128,128]{2,1,0:T(8,128)(2,1)}), bf16[8,128,128]{2,1,0:T(8,128)(2,1)S(1)}, u32[]{:S(2)}, u32[]{:S(2)}) %all-to-all-start) | async-done | bytes 262176 | tf_op jit(solution)/shard_map/all_to_all | solution.py:402
  31.2 1.4 collective-permute-start.1
  32.6 2.6 %collective-permute-start.2 = (bf16[32,128]{1,0:T(8,128)(2,1)S(1)}, bf16[32,128]{1,0:T(8,128)(2,1)S(1)}, u32[]{:S(2)}, u32[]{:S(2)}) collective-permute-start(bf16[32,128]{1,0:T(8,128)(2,1)S(1)} %get-tuple-element.34), channel_id=1, source_target_pairs={{0,128},{16,144},{32,160},{48,176},{64,192},{80,208},{96,224},{112... | collective-permute-start | bytes 24584 | tf_op jit(solution)/shard_map/ppermute | solution.py:406
  36.3 5.3 %collective-permute-done.5.refs_6_ = bf16[2,2,32,8,128]{4,3,2,1,0:T(8,128)(2,1)S(1)} collective-permute-done((bf16[2,2,32,8,128]{4,3,2,1,0:T(8,128)(2,1)S(1)}, bf16[2,2,32,8,128]{4,3,2,1,0:T(8,128)(2,1)S(1)}, u32[]{:S(2)}, u32[]{:S(2)}) %collective-permute-start.5) | collective-permute-done | bytes 262176 | tf_op jit(solution)/shard_map/ppermute | solution.py:383
  42.5 2.8 %collective-permute-start.7 = (bf16[128,128]{1,0:T(8,128)(2,1)S(1)}, bf16[128,128]{1,0:T(8,128)(2,1)S(1)}, u32[]{:S(2)}, u32[]{:S(2)}) collective-permute-start(bf16[128,128]{1,0:T(8,128)(2,1)S(1)} %get-tuple-element.38), channel_id=1, source_target_pairs={{0,192},{16,208},{32,224},{48,240},{64,0},{80,16},{96,32},{112,48}... | collective-permute-start | bytes 98312 | tf_op jit(solution)/shard_map/ppermute | solution.py:419
  46.4 3.2 %collective-permute-done.8.refs_2_ = bf16[128,128]{1,0:T(8,128)(2,1)S(1)} collective-permute-done((bf16[128,128]{1,0:T(8,128)(2,1)S(1)}, bf16[128,128]{1,0:T(8,128)(2,1)S(1)}, u32[]{:S(2)}, u32[]{:S(2)}) %collective-permute-start.8) | collective-permute-done | bytes 32800 | tf_op jit(solution)/shard_map/ppermute | solution.py:419
  50.0 14.6 %all_to_all.30.own_ref = bf16[8,128,128]{2,1,0:T(8,128)(2,1)S(1)} all-to-all(bf16[8,128,128]{2,1,0:T(8,128)(2,1)S(1)} %shard_map.50), channel_id=1, replica_groups={{0,1,2,3,8,9,10,11},{4,5,6,7,12,13,14,15},{16,17,18,19,24,25,26,27},{20..., dimensions={0} | all-to-all | bytes 524288 | tf_op jit(solution)/shard_map/all_to_all | solution.py:433
  64.6 4.6 %collective-permute-start.10 = (bf16[8,128,128]{2,1,0:T(8,128)(2,1)S(1)}, bf16[8,128,128]{2,1,0:T(8,128)(2,1)S(1)}, u32[]{:S(2)}, u32[]{:S(2)}) collective-permute-start(bf16[8,128,128]{2,1,0:T(8,128)(2,1)S(1)} %all_to_all.30.own_ref), channel_id=1, source_target_pairs={{0,4},{4,0},{1,5},{5,1},{2,6},{6,2},{3,7},{7,3},{8,12},{12,8},{9,1... | collective-permute-start | bytes 786440 | tf_op jit(solution)/shard_map/ppermute | solution.py:437
  70.4 5.6 %shard_map.51 = (bf16[128,128,128]{2,1,0:T(8,128)(2,1)}, f32[8,128,128]{2,1,0:T(8,128)S(1)}, bf16[8,128,128]{2,1,0:T(8,128)(2,1)S(1)}) custom-call(bf16[128,128,128]{2,1,0:T(8,128)(2,1)} %bitcast.11, bf16[8,128,128]{2,1,0:T(8,128)(2,1)S(1)} %all_to_all.30.own_ref, bf16[8,128,128]{2,1,0:T(8,128)(2,1)S(1)} %collective-permute-done.10.oth_ref, ...), custom_call_target="tpu_custom_call" | custom-call | tf_op jit(solution)/shard_map/pallas_call | solution.py:346
  77.7 12.9 %all_to_all.31 = bf16[8,128,128]{2,1,0:T(8,128)(2,1)S(1)} all-to-all(bf16[8,128,128]{2,1,0:T(8,128)(2,1)S(1)} %add_convert_fusion.1), channel_id=1, replica_groups={{0,1,2,3,8,9,10,11},{4,5,6,7,12,13,14,15},{16,17,18,19,24,25,26,27},{20..., dimensions={0} | all-to-all | bytes 524288 | tf_op jit(solution)/shard_map/all_to_all | solution.py:402
  90.6 3.2 %shard_map.52 = bf16[8,128,128]{2,1,0:T(8,128)(2,1)S(1)} custom-call(bf16[128,128]{1,0:T(8,128)(2,1)S(1)} %reduce_sum.24.a_ref, bf16[16,2,2,32,8,128]{5,4,3,2,1,0:T(8,128)(2,1)} %bitcast.12), custom_call_target="tpu_custom_call" | custom-call | tf_op jit(solution)/shard_map/pallas_call | solution.py:346
  93.8 14.5 %all_to_all.32.own_ref = bf16[8,128,128]{2,1,0:T(8,128)(2,1)S(1)} all-to-all(bf16[8,128,128]{2,1,0:T(8,128)(2,1)S(1)} %shard_map.52), channel_id=1, replica_groups={{0,1,2,3,8,9,10,11},{4,5,6,7,12,13,14,15},{16,17,18,19,24,25,26,27},{20..., dimensions={0} | all-to-all | bytes 524288 | tf_op jit(solution)/shard_map/all_to_all | solution.py:433
  108.3 2.9 %collective-permute-start.12 = (bf16[8,128,128]{2,1,0:T(8,128)(2,1)S(1)}, bf16[8,128,128]{2,1,0:T(8,128)(2,1)S(1)}, u32[]{:S(2)}, u32[]{:S(2)}) collective-permute-start(bf16[8,128,128]{2,1,0:T(8,128)(2,1)S(1)} %all_to_all.32.own_ref), channel_id=1, source_target_pairs={{0,4},{4,0},{1,5},{5,1},{2,6},{6,2},{3,7},{7,3},{8,12},{12,8},{9,1... | collective-permute-start | bytes 786440 | tf_op jit(solution)/shard_map/ppermute | solution.py:437
  112.4 6.0 %shard_map.53 = (bf16[128,128,128]{2,1,0:T(8,128)(2,1)}, f32[8,128,128]{2,1,0:T(8,128)S(1)}, bf16[8,128,128]{2,1,0:T(8,128)(2,1)S(1)}) custom-call(bf16[128,128,128]{2,1,0:T(8,128)(2,1)} %get-tuple-element.47.u_hbm, bf16[8,128,128]{2,1,0:T(8,128)(2,1)S(1)} %all_to_all.32.own_ref, bf16[8,128,128]{2,1,0:T(8,128)(2,1)S(1)} %collective-permute-done.12.oth_ref, ...), custom_call_target="tpu_custom_call" | custom-call | tf_op jit(solution)/shard_map/pallas_call | solution.py:346
  120.1 12.3 %all_to_all.33 = bf16[8,128,128]{2,1,0:T(8,128)(2,1)S(1)} all-to-all(bf16[8,128,128]{2,1,0:T(8,128)(2,1)S(1)} %add_convert_fusion), channel_id=1, replica_groups={{0,1,2,3,8,9,10,11},{4,5,6,7,12,13,14,15},{16,17,18,19,24,25,26,27},{20..., dimensions={0} | all-to-all | bytes 524288 | tf_op jit(solution)/shard_map/all_to_all | solution.py:402
  132.8 3.2 %shard_map.54 = bf16[8,128,128]{2,1,0:T(8,128)(2,1)S(1)} custom-call(bf16[128,128]{1,0:T(8,128)(2,1)S(1)} %reduce_sum.25.a_ref, bf16[16,2,2,32,8,128]{5,4,3,2,1,0:T(8,128)(2,1)} %bitcast.13), custom_call_target="tpu_custom_call" | custom-call | tf_op jit(solution)/shard_map/pallas_call | solution.py:346
  136.0 15.1 %all_to_all.34.own_ref = bf16[8,128,128]{2,1,0:T(8,128)(2,1)S(1)} all-to-all(bf16[8,128,128]{2,1,0:T(8,128)(2,1)S(1)} %shard_map.54), channel_id=1, replica_groups={{0,1,2,3,8,9,10,11},{4,5,6,7,12,13,14,15},{16,17,18,19,24,25,26,27},{20..., dimensions={0} | all-to-all | bytes 524288 | tf_op jit(solution)/shard_map/all_to_all | solution.py:433
  151.1 3.3 %collective-permute-start.14 = (bf16[8,128,128]{2,1,0:T(8,128)(2,1)S(1)}, bf16[8,128,128]{2,1,0:T(8,128)(2,1)S(1)}, u32[]{:S(2)}, u32[]{:S(2)}) collective-permute-start(bf16[8,128,128]{2,1,0:T(8,128)(2,1)S(1)} %all_to_all.34.own_ref), channel_id=1, source_target_pairs={{0,4},{4,0},{1,5},{5,1},{2,6},{6,2},{3,7},{7,3},{8,12},{12,8},{9,1... | collective-permute-start | bytes 786440 | tf_op jit(solution)/shard_map/ppermute | solution.py:437
  155.5 5.1 %shard_map.55 = bf16[128,128,128]{2,1,0:T(8,128)(2,1)} custom-call(bf16[128,128,128]{2,1,0:T(8,128)(2,1)} %get-tuple-element.51.u_hbm, bf16[8,128,128]{2,1,0:T(8,128)(2,1)S(1)} %all_to_all.34.own_ref, bf16[8,128,128]{2,1,0:T(8,128)(2,1)S(1)} %collective-permute-done.14.oth_ref, bf16[256,64]{1,0:T(8,128)(2,1)S(1)} %get-tuple-element.43.ix_ref, ...), custom_call_target="tpu_custom_call" | custom-call | tf_op jit(solution)/shard_map/pallas_call | solution.py:346
  (47 shorter events, 15.1 us)
Async XLA Ops:
  6.5 84.1 %all-gather.5.cloned.1.call-start = ((), (), s32[]{:S(2)}) async-start(), calls=%async_computation.6 | async-start | bytes 4456448 | tf_op jit(solution)/shard_map/all_gather | solution.py:378
  8.8 60.4 %copy-start.1 = (f32[3,128]{1,0:T(4,128)S(1)}, f32[3,128]{1,0:T(4,128)}, u32[]{:S(2)}) copy-start(f32[3,128]{1,0:T(4,128)} %param.7) | copy-start | bytes 4612
  8.8 60.4 %copy-start = (bf16[3,128,128]{2,1,0:T(8,128)(2,1)S(1)}, bf16[3,128,128]{2,1,0:T(8,128)(2,1)}, u32[]{:S(2)}) copy-start(bf16[3,128,128]{2,1,0:T(8,128)(2,1)} %param.6) | copy-start | bytes 294916
  11.9 1.9 %collective-permute-start = (bf16[8,128,128]{2,1,0:T(8,128)(2,1)S(1)}, bf16[8,128,128]{2,1,0:T(8,128)(2,1)S(1)}, u32[]{:S(2)}, u32[]{:S(2)}) collective-permute-start(bf16[8,128,128]{2,1,0:T(8,128)(2,1)S(1)} %get-tuple-element.31), channel_id=1, source_target_pairs={{0,4},{4,0},{1,5},{5,1},{2,6},{6,2},{3,7},{7,3},{8,12},{12,8},{9,1... | collective-permute-start | bytes 786440 | tf_op jit(solution)/shard_map/ppermute | solution.py:400
  14.6 16.5 %all-to-all-start = ((bf16[8,128,128]{2,1,0:T(8,128)(2,1)}), bf16[8,128,128]{2,1,0:T(8,128)(2,1)S(1)}, u32[]{:S(2)}, u32[]{:S(2)}) async-start(bf16[8,128,128]{2,1,0:T(8,128)(2,1)} %add_convert_fusion.2), calls=%async_computation | async-start | bytes 524288 | tf_op jit(solution)/shard_map/all_to_all | solution.py:402
  22.6 110.2 %all-gather.7.cloned.1.call-start = ((), (), s32[]{:S(2)}) async-start(), calls=%async_computation.7 | async-start | bytes 4456448 | tf_op jit(solution)/shard_map/all_gather | solution.py:378
  22.6 12.6 %collective-permute-start.4 = (bf16[2,2,32,8,128]{4,3,2,1,0:T(8,128)(2,1)S(1)}, bf16[2,2,32,8,128]{4,3,2,1,0:T(8,128)(2,1)S(1)}, u32[]{:S(2)}, u32[]{:S(2)}) collective-permute-start(bf16[2,2,32,8,128]{4,3,2,1,0:T(8,128)(2,1)S(1)} %get-tuple-element.36.refs_4_), channel_id=1, source_target_pairs={{0,16},{16,32},{32,48},{48,0},{64,80},{80,96},{96,112},{112,64},{1... | collective-permute-start | bytes 786440 | tf_op jit(solution)/shard_map/ppermute | solution.py:383
  23.8 17.7 %collective-permute-start.5 = (bf16[2,2,32,8,128]{4,3,2,1,0:T(8,128)(2,1)S(1)}, bf16[2,2,32,8,128]{4,3,2,1,0:T(8,128)(2,1)S(1)}, u32[]{:S(2)}, u32[]{:S(2)}) collective-permute-start(bf16[2,2,32,8,128]{4,3,2,1,0:T(8,128)(2,1)S(1)} %get-tuple-element.36.refs_4_), channel_id=1, source_target_pairs={{0,32},{16,48},{32,0},{48,16},{64,96},{80,112},{96,64},{112,80},{1... | collective-permute-start | bytes 786440 | tf_op jit(solution)/shard_map/ppermute | solution.py:383
  26.3 15.3 %collective-permute-start.6 = (bf16[2,2,32,8,128]{4,3,2,1,0:T(8,128)(2,1)S(1)}, bf16[2,2,32,8,128]{4,3,2,1,0:T(8,128)(2,1)S(1)}, u32[]{:S(2)}, u32[]{:S(2)}) collective-permute-start(bf16[2,2,32,8,128]{4,3,2,1,0:T(8,128)(2,1)S(1)} %get-tuple-element.36.refs_4_), channel_id=1, source_target_pairs={{0,48},{16,0},{32,16},{48,32},{64,112},{80,64},{96,80},{112,96},{1... | collective-permute-start | bytes 786440 | tf_op jit(solution)/shard_map/ppermute | solution.py:383
  31.2 10.3 %collective-permute-start.1 = (bf16[32,128]{1,0:T(8,128)(2,1)S(1)}, bf16[32,128]{1,0:T(8,128)(2,1)S(1)}, u32[]{:S(2)}, u32[]{:S(2)}) collective-permute-start(bf16[32,128]{1,0:T(8,128)(2,1)S(1)} %get-tuple-element.33), channel_id=1, source_target_pairs={{0,64},{16,80},{32,96},{48,112},{64,128},{80,144},{96,160},{112,17... | collective-permute-start | bytes 24584 | tf_op jit(solution)/shard_map/ppermute | solution.py:406
  32.6 9.0 %collective-permute-start.2 = (bf16[32,128]{1,0:T(8,128)(2,1)S(1)}, bf16[32,128]{1,0:T(8,128)(2,1)S(1)}, u32[]{:S(2)}, u32[]{:S(2)}) collective-permute-start(bf16[32,128]{1,0:T(8,128)(2,1)S(1)} %get-tuple-element.34), channel_id=1, source_target_pairs={{0,128},{16,144},{32,160},{48,176},{64,192},{80,208},{96,224},{112... | collective-permute-start | bytes 24584 | tf_op jit(solution)/shard_map/ppermute | solution.py:406
  35.2 6.3 %collective-permute-start.3 = (bf16[32,128]{1,0:T(8,128)(2,1)S(1)}, bf16[32,128]{1,0:T(8,128)(2,1)S(1)}, u32[]{:S(2)}, u32[]{:S(2)}) collective-permute-start(bf16[32,128]{1,0:T(8,128)(2,1)S(1)} %get-tuple-element.35), channel_id=1, source_target_pairs={{0,192},{16,208},{32,224},{48,240},{64,0},{80,16},{96,32},{112,48}... | collective-permute-start | bytes 24584 | tf_op jit(solution)/shard_map/ppermute | solution.py:406
  42.5 3.9 %collective-permute-start.7 = (bf16[128,128]{1,0:T(8,128)(2,1)S(1)}, bf16[128,128]{1,0:T(8,128)(2,1)S(1)}, u32[]{:S(2)}, u32[]{:S(2)}) collective-permute-start(bf16[128,128]{1,0:T(8,128)(2,1)S(1)} %get-tuple-element.38), channel_id=1, source_target_pairs={{0,192},{16,208},{32,224},{48,240},{64,0},{80,16},{96,32},{112,48}... | collective-permute-start | bytes 98312 | tf_op jit(solution)/shard_map/ppermute | solution.py:419
  45.3 4.3 %collective-permute-start.8 = (bf16[128,128]{1,0:T(8,128)(2,1)S(1)}, bf16[128,128]{1,0:T(8,128)(2,1)S(1)}, u32[]{:S(2)}, u32[]{:S(2)}) collective-permute-start(bf16[128,128]{1,0:T(8,128)(2,1)S(1)} %get-tuple-element.39), channel_id=1, source_target_pairs={{0,128},{16,144},{32,160},{48,176},{64,192},{80,208},{96,224},{112... | collective-permute-start | bytes 98312 | tf_op jit(solution)/shard_map/ppermute | solution.py:419
  45.7 4.3 %collective-permute-start.9 = (bf16[128,128]{1,0:T(8,128)(2,1)S(1)}, bf16[128,128]{1,0:T(8,128)(2,1)S(1)}, u32[]{:S(2)}, u32[]{:S(2)}) collective-permute-start(bf16[128,128]{1,0:T(8,128)(2,1)S(1)} %get-tuple-element.40), channel_id=1, source_target_pairs={{0,64},{16,80},{32,96},{48,112},{64,128},{80,144},{96,160},{112,17... | collective-permute-start | bytes 98312 | tf_op jit(solution)/shard_map/ppermute | solution.py:419
  64.6 5.8 %collective-permute-start.10 = (bf16[8,128,128]{2,1,0:T(8,128)(2,1)S(1)}, bf16[8,128,128]{2,1,0:T(8,128)(2,1)S(1)}, u32[]{:S(2)}, u32[]{:S(2)}) collective-permute-start(bf16[8,128,128]{2,1,0:T(8,128)(2,1)S(1)} %all_to_all.30.own_ref), channel_id=1, source_target_pairs={{0,4},{4,0},{1,5},{5,1},{2,6},{6,2},{3,7},{7,3},{8,12},{12,8},{9,1... | collective-permute-start | bytes 786440 | tf_op jit(solution)/shard_map/ppermute | solution.py:437
  76.0 1.6 collective-permute-start.11
  108.3 4.1 %collective-permute-start.12 = (bf16[8,128,128]{2,1,0:T(8,128)(2,1)S(1)}, bf16[8,128,128]{2,1,0:T(8,128)(2,1)S(1)}, u32[]{:S(2)}, u32[]{:S(2)}) collective-permute-start(bf16[8,128,128]{2,1,0:T(8,128)(2,1)S(1)} %all_to_all.32.own_ref), channel_id=1, source_target_pairs={{0,4},{4,0},{1,5},{5,1},{2,6},{6,2},{3,7},{7,3},{8,12},{12,8},{9,1... | collective-permute-start | bytes 786440 | tf_op jit(solution)/shard_map/ppermute | solution.py:437
  118.4 1.6 collective-permute-start.13
  151.1 4.4 %collective-permute-start.14 = (bf16[8,128,128]{2,1,0:T(8,128)(2,1)S(1)}, bf16[8,128,128]{2,1,0:T(8,128)(2,1)S(1)}, u32[]{:S(2)}, u32[]{:S(2)}) collective-permute-start(bf16[8,128,128]{2,1,0:T(8,128)(2,1)S(1)} %all_to_all.34.own_ref), channel_id=1, source_target_pairs={{0,4},{4,0},{1,5},{5,1},{2,6},{6,2},{3,7},{7,3},{8,12},{12,8},{9,1... | collective-permute-start | bytes 786440 | tf_op jit(solution)/shard_map/ppermute | solution.py:437
Sparse Core Ops, SparseCore 0:
  9.8 64.2 all-gather.4
  76.5 56.2 all-gather.6
